TPU v7x, 8 devices: a whole 2x2x1 slice. The times are simulated.
8 devices in a mesh: dp: 1 (over z), cpo: 2 (over y), cp: 4 (over x, core).
Axes of the slice: x: 2, y: 2, z: 1, core: 2. Of those that a mesh axis runs over, the one named last changes fastest.
Arguments:
- queries: bfloat16 [4096, 2, 128], P(('dp', 'cpo', 'cp'))
- keys: bfloat16 [4096, 128], P(('dp', 'cpo', 'cp'))
- values: bfloat16 [4096, 128], P(('dp', 'cpo', 'cp'))
- attn_out: bfloat16 [4096, 2, 128], P(('dp', 'cpo', 'cp'))
- logsumexp: float32 [4096, 2], P(('dp', 'cpo', 'cp'))
- d_out: bfloat16 [4096, 2, 128], P(('dp', 'cpo', 'cp'))
- cu_seqlens: int32 [14], P('dp')
Outputs:
- output 1: bfloat16 [4096, 2, 128], P(('dp', 'cpo', 'cp'))
- output 2: bfloat16 [4096, 128], P(('dp', 'cpo', 'cp'))
- output 3: bfloat16 [4096, 128], P(('dp', 'cpo', 'cp'))
All inputs are finite; a program needn't handle non-finite values.
Results may differ from a plain program's by a relative error of at most 0.001.
Values are sent between devices in bfloat16 or wider.
A program may use at most 1 GiB of HBM per device.

v0:
```python
import jax
import jax.numpy as jnp
from jax import lax
from jax.sharding import PartitionSpec as P

HOPS = 3


def doc_ids(bounds, positions, seq_len):
    found = jnp.searchsorted(bounds[1:], positions, side="right").astype(jnp.int32)
    return jnp.where((positions >= 0) & (positions < seq_len), found, -1)


def window_backward(q_loc, do_loc, lse_loc, dot_loc, id_q, pos_q, k_win, v_win, id_k, pos_k, scale):
    rows, heads, head = q_loc.shape
    block_rows = min(64, rows)
    count = rows // block_rows
    blocks = (
        q_loc.reshape(count, block_rows, heads, head),
        do_loc.reshape(count, block_rows, heads, head),
        lse_loc.reshape(count, block_rows, heads),
        dot_loc.reshape(count, block_rows, heads),
        id_q.reshape(count, block_rows),
        pos_q.reshape(count, block_rows),
    )

    def step(carry, block):
        dk_acc, dv_acc = carry
        q_blk, do_blk, lse_blk, dot_blk, idq_blk, posq_blk = block
        keep = (idq_blk[:, None] == id_k[None, :]) & (pos_k[None, :] <= posq_blk[:, None])
        scores = jnp.einsum("qgd,kd->qgk", q_blk, k_win, preferred_element_type=jnp.float32)
        p_mat = jnp.where(keep[:, None, :], jnp.exp(scale * scores - lse_blk[:, :, None]), 0.0)
        dp_mat = jnp.einsum("qgd,kd->qgk", do_blk, v_win, preferred_element_type=jnp.float32)
        ds_mat = (p_mat * (dp_mat - dot_blk[:, :, None])).astype(jnp.bfloat16)
        dq_blk = scale * jnp.einsum("qgk,kd->qgd", ds_mat, k_win, preferred_element_type=jnp.float32)
        dk_acc = dk_acc + jnp.einsum("qgk,qgd->kd", ds_mat, q_blk, preferred_element_type=jnp.float32)
        dv_acc = dv_acc + jnp.einsum("qgk,qgd->kd", p_mat.astype(jnp.bfloat16), do_blk, preferred_element_type=jnp.float32)
        return (dk_acc, dv_acc), dq_blk.astype(jnp.bfloat16)

    width = k_win.shape[0]
    init = (jnp.zeros((width, head), jnp.float32), jnp.zeros((width, head), jnp.float32))
    (dk_sum, dv_sum), dq_blocks = lax.scan(step, init, blocks)
    return dq_blocks.reshape(rows, heads, head), dk_sum, dv_sum


def solution(mesh):
    inner = mesh.shape["cp"]
    group = mesh.shape["cpo"] * inner
    seq_axes = ("cpo", "cp")

    def local(queries, keys, values, attn_out, logsumexp, d_out, cu_seqlens):
        rows, heads, head = queries.shape
        scale = head ** -0.5
        seq_len = group * rows
        rank = lax.axis_index("cpo") * inner + lax.axis_index("cp")
        kv_pair = jnp.stack([keys, values])
        received = []
        for hop in range(HOPS, 0, -1):
            received.append(lax.ppermute(kv_pair, seq_axes, [(sender, sender + hop) for sender in range(group - hop)]))
        received.append(kv_pair)
        kv_win = jnp.concatenate(received, axis=1)
        pos_q = rank * rows + jnp.arange(rows, dtype=jnp.int32)
        pos_k = (rank - HOPS) * rows + jnp.arange((HOPS + 1) * rows, dtype=jnp.int32)
        id_q = doc_ids(cu_seqlens, pos_q, seq_len)
        id_k = doc_ids(cu_seqlens, pos_k, seq_len)
        row_dot = jnp.einsum("qgd,qgd->qg", d_out, attn_out, preferred_element_type=jnp.float32)
        d_query, dk_sum, dv_sum = window_backward(queries, d_out, logsumexp, row_dot, id_q, pos_q, kv_win[0], kv_win[1], id_k, pos_k, scale)
        part_sums = jnp.stack([dk_sum, dv_sum]).reshape(2, HOPS + 1, rows, head)
        owned = part_sums[:, HOPS]
        for hop in range(1, HOPS + 1):
            owned = owned + lax.ppermute(part_sums[:, HOPS - hop], seq_axes, [(sender, sender - hop) for sender in range(hop, group)])
        return d_query, (scale * owned[0]).astype(jnp.bfloat16), owned[1].astype(jnp.bfloat16)

    seq_spec = P(("dp", "cpo", "cp"))
    return jax.shard_map(local, mesh=mesh, in_specs=(seq_spec, seq_spec, seq_spec, seq_spec, seq_spec, seq_spec, P("dp")), out_specs=(seq_spec, seq_spec, seq_spec), check_vma=False)
```

profile of v0, /device:TPU:3, one launch (start us, length us, event | category | flops | bytes accessed | tf_op | source)
XLA Modules:
  0.0 162.1 jit_solution(4012725691275806305)
XLA Ops:
  0.7 1.1 pad_maximum_fusion.1
  1.7 3.7 %collective-permute-start = (bf16[2,512,128]{2,1,0:T(8,128)(2,1)S(1)}, bf16[2,512,128]{2,1,0:T(8,128)(2,1)S(1)}, u32[]{:S(2)}, u32[]{:S(2)}) collective-permute-start(bf16[2,512,128]{2,1,0:T(8,128)(2,1)S(1)} %pad_maximum_fusion.1), channel_id=1, source_target_pairs={{0,3},{1,4},{2,5},{3,6},{4,7}} | collective-permute-start | bytes 786440 | tf_op jit(solution)/shard_map/ppermute | solution.py:59
  5.4 1.9 %collective-permute-start.1 = (bf16[2,512,128]{2,1,0:T(8,128)(2,1)S(1)}, bf16[2,512,128]{2,1,0:T(8,128)(2,1)S(1)}, u32[]{:S(2)}, u32[]{:S(2)}) collective-permute-start(bf16[2,512,128]{2,1,0:T(8,128)(2,1)S(1)} %pad_maximum_fusion.1), channel_id=1, source_target_pairs={{0,2},{1,3},{2,4},{3,5},{4,6},{5,7}} | collective-permute-start | bytes 786440 | tf_op jit(solution)/shard_map/ppermute | solution.py:59
  7.3 2.8 %collective-permute-start.2 = (bf16[2,512,128]{2,1,0:T(8,128)(2,1)S(1)}, bf16[2,512,128]{2,1,0:T(8,128)(2,1)S(1)}, u32[]{:S(2)}, u32[]{:S(2)}) collective-permute-start(bf16[2,512,128]{2,1,0:T(8,128)(2,1)S(1)} %pad_maximum_fusion.1), channel_id=1, source_target_pairs={{0,1},{1,2},{2,3},{3,4},{4,5},{5,6},{6,7}} | collective-permute-start | bytes 786440 | tf_op jit(solution)/shard_map/ppermute | solution.py:59
  11.0 35.6 %while.64 = (s32[]{:T(128)}, u32[2048]{0:T(1024)S(1)}, u32[2048]{0:T(1024)S(1)}, s32[13]{0:T(128)S(1)}, s32[]{:T(128)}, /*index=5*/s32[]{:T(128)}, s32[]{:T(128)}) while((s32[]{:T(128)}, u32[2048]{0:T(1024)S(1)}, u32[2048]{0:T(1024)S(1)}, s32[13]{0:T(128)S(1)}, s32[]{:T(128)}, /*index=5*/s32[]{:T(128)}, s32[]{:T(128)}) %tuple.123), condition=%wide.region_3.4_spmd.clone, body=%wide.region_2.3_spmd.clone.sunk | while | flops 67587 | bytes 33015 | solution.py:10
  11.7 8.2 %fusion.70 = (u32[2048]{0:T(1024)S(1)}, u32[2048]{0:T(1024)S(1)}) fusion(u32[2048]{0:T(1024)S(1)} %get-tuple-element.648, u32[2048]{0:T(1024)S(1)} %get-tuple-element.647, s32[]{:T(128)} %get-tuple-element.657, s32[]{:T(128)} %bitcast.149, s32[]{:T(128)} %bitcast.150, s32[]{:T(128)} %bitcast.151, s32[]{:T(128)} %bitcast.152, s32[]{:T(128)} %bitcast.153, ...), kind=kLoop, calls=%fused_computation.8.clone.1 | loop fusion | flops 67584 | bytes 32825 | tf_op jit(solution)/shard_map/jit(searchsorted)/jit(_searchsorted_scan_impl)/vmap(jit(_searchsorted_scan_impl))/while/body/eval_jaxpr/select_n | solution.py:10
  20.6 8.2 %fusion.70 = (u32[2048]{0:T(1024)S(1)}, u32[2048]{0:T(1024)S(1)}) fusion(u32[2048]{0:T(1024)S(1)} %get-tuple-element.648, u32[2048]{0:T(1024)S(1)} %get-tuple-element.647, s32[]{:T(128)} %get-tuple-element.657, s32[]{:T(128)} %bitcast.149, s32[]{:T(128)} %bitcast.150, s32[]{:T(128)} %bitcast.151, s32[]{:T(128)} %bitcast.152, s32[]{:T(128)} %bitcast.153, ...), kind=kLoop, calls=%fused_computation.8.clone.1 | loop fusion | flops 67584 | bytes 32825 | tf_op jit(solution)/shard_map/jit(searchsorted)/jit(_searchsorted_scan_impl)/vmap(jit(_searchsorted_scan_impl))/while/body/eval_jaxpr/select_n | solution.py:10
  29.5 8.2 %fusion.70 = (u32[2048]{0:T(1024)S(1)}, u32[2048]{0:T(1024)S(1)}) fusion(u32[2048]{0:T(1024)S(1)} %get-tuple-element.648, u32[2048]{0:T(1024)S(1)} %get-tuple-element.647, s32[]{:T(128)} %get-tuple-element.657, s32[]{:T(128)} %bitcast.149, s32[]{:T(128)} %bitcast.150, s32[]{:T(128)} %bitcast.151, s32[]{:T(128)} %bitcast.152, s32[]{:T(128)} %bitcast.153, ...), kind=kLoop, calls=%fused_computation.8.clone.1 | loop fusion | flops 67584 | bytes 32825 | tf_op jit(solution)/shard_map/jit(searchsorted)/jit(_searchsorted_scan_impl)/vmap(jit(_searchsorted_scan_impl))/while/body/eval_jaxpr/select_n | solution.py:10
  38.4 8.2 %fusion.70 = (u32[2048]{0:T(1024)S(1)}, u32[2048]{0:T(1024)S(1)}) fusion(u32[2048]{0:T(1024)S(1)} %get-tuple-element.648, u32[2048]{0:T(1024)S(1)} %get-tuple-element.647, s32[]{:T(128)} %get-tuple-element.657, s32[]{:T(128)} %bitcast.149, s32[]{:T(128)} %bitcast.150, s32[]{:T(128)} %bitcast.151, s32[]{:T(128)} %bitcast.152, s32[]{:T(128)} %bitcast.153, ...), kind=kLoop, calls=%fused_computation.8.clone.1 | loop fusion | flops 67584 | bytes 32825 | tf_op jit(solution)/shard_map/jit(searchsorted)/jit(_searchsorted_scan_impl)/vmap(jit(_searchsorted_scan_impl))/while/body/eval_jaxpr/select_n | solution.py:10
  46.6 36.0 %while.63 = (s32[]{:T(128)}, u32[512]{0:T(512)S(1)}, u32[512]{0:T(512)S(1)}, s32[13]{0:T(128)S(1)}, s32[]{:T(128)}, /*index=5*/s32[]{:T(128)}, s32[]{:T(128)}) while((s32[]{:T(128)}, u32[512]{0:T(512)S(1)}, u32[512]{0:T(512)S(1)}, s32[13]{0:T(128)S(1)}, s32[]{:T(128)}, /*index=5*/s32[]{:T(128)}, s32[]{:T(128)}) %tuple.129), condition=%wide.region_1.2_spmd.clone, body=%wide.region_0.1_spmd.clone.sunk | while | flops 16899 | bytes 8439 | solution.py:10
  47.3 8.3 %fusion.68 = (u32[512]{0:T(512)S(1)}, u32[512]{0:T(512)S(1)}) fusion(u32[512]{0:T(512)S(1)} %get-tuple-element.627, u32[512]{0:T(512)S(1)} %get-tuple-element.626, s32[]{:T(128)} %get-tuple-element.636, s32[]{:T(128)} %bitcast.136, s32[]{:T(128)} %bitcast.137, s32[]{:T(128)} %bitcast.138, s32[]{:T(128)} %bitcast.139, s32[]{:T(128)} %bitcast.140, ...), kind=kLoop, calls=%fused_computation.5.clone.1 | loop fusion | flops 16896 | bytes 8249 | tf_op jit(solution)/shard_map/jit(searchsorted)/jit(_searchsorted_scan_impl)/vmap(jit(_searchsorted_scan_impl))/while/body/eval_jaxpr/select_n | solution.py:10
  56.3 8.3 %fusion.68 = (u32[512]{0:T(512)S(1)}, u32[512]{0:T(512)S(1)}) fusion(u32[512]{0:T(512)S(1)} %get-tuple-element.627, u32[512]{0:T(512)S(1)} %get-tuple-element.626, s32[]{:T(128)} %get-tuple-element.636, s32[]{:T(128)} %bitcast.136, s32[]{:T(128)} %bitcast.137, s32[]{:T(128)} %bitcast.138, s32[]{:T(128)} %bitcast.139, s32[]{:T(128)} %bitcast.140, ...), kind=kLoop, calls=%fused_computation.5.clone.1 | loop fusion | flops 16896 | bytes 8249 | tf_op jit(solution)/shard_map/jit(searchsorted)/jit(_searchsorted_scan_impl)/vmap(jit(_searchsorted_scan_impl))/while/body/eval_jaxpr/select_n | solution.py:10
  65.3 8.3 %fusion.68 = (u32[512]{0:T(512)S(1)}, u32[512]{0:T(512)S(1)}) fusion(u32[512]{0:T(512)S(1)} %get-tuple-element.627, u32[512]{0:T(512)S(1)} %get-tuple-element.626, s32[]{:T(128)} %get-tuple-element.636, s32[]{:T(128)} %bitcast.136, s32[]{:T(128)} %bitcast.137, s32[]{:T(128)} %bitcast.138, s32[]{:T(128)} %bitcast.139, s32[]{:T(128)} %bitcast.140, ...), kind=kLoop, calls=%fused_computation.5.clone.1 | loop fusion | flops 16896 | bytes 8249 | tf_op jit(solution)/shard_map/jit(searchsorted)/jit(_searchsorted_scan_impl)/vmap(jit(_searchsorted_scan_impl))/while/body/eval_jaxpr/select_n | solution.py:10
  74.3 8.3 %fusion.68 = (u32[512]{0:T(512)S(1)}, u32[512]{0:T(512)S(1)}) fusion(u32[512]{0:T(512)S(1)} %get-tuple-element.627, u32[512]{0:T(512)S(1)} %get-tuple-element.626, s32[]{:T(128)} %get-tuple-element.636, s32[]{:T(128)} %bitcast.136, s32[]{:T(128)} %bitcast.137, s32[]{:T(128)} %bitcast.138, s32[]{:T(128)} %bitcast.139, s32[]{:T(128)} %bitcast.140, ...), kind=kLoop, calls=%fused_computation.5.clone.1 | loop fusion | flops 16896 | bytes 8249 | tf_op jit(solution)/shard_map/jit(searchsorted)/jit(_searchsorted_scan_impl)/vmap(jit(_searchsorted_scan_impl))/while/body/eval_jaxpr/select_n | solution.py:10
  83.7 0.9 slice_bitcast_fusion
  84.6 40.9 %while.65 = (s32[]{:T(128)}, f32[2048,128]{1,0:T(8,128)S(1)}, f32[2048,128]{1,0:T(8,128)}, bf16[8,64,2,128]{3,2,1,0:T(2,128)(2,1)}, s32[8,64]{1,0:T(8,128)S(1)},...) while((s32[]{:T(128)}, f32[2048,128]{1,0:T(8,128)S(1)}, ...), condition=%wide.region_5.6_spmd.clone, body=%wide.region_4.5_spmd.clone.sunk | while | flops 338855936 | bytes 21624072 | solution.py:42
  84.8 0.8 constant_dynamic-slice_fusion.9
  125.5 1.3 fusion.34
  126.8 2.3 %collective-permute-start.3 = (f32[2,512,128]{2,1,0:T(8,128)S(1)}, f32[2,512,128]{2,1,0:T(8,128)S(1)}, u32[]{:S(2)}, u32[]{:S(2)}) collective-permute-start(f32[2,512,128]{2,1,0:T(8,128)S(1)} %get-tuple-element.398), channel_id=1, source_target_pairs={{1,0},{2,1},{3,2},{4,3},{5,4},{6,5},{7,6}} | collective-permute-start | bytes 1572872 | tf_op jit(solution)/shard_map/ppermute | solution.py:71
  129.1 3.2 %collective-permute-start.4 = (f32[2,512,128]{2,1,0:T(8,128)S(1)}, f32[2,512,128]{2,1,0:T(8,128)S(1)}, u32[]{:S(2)}, u32[]{:S(2)}) collective-permute-start(f32[2,512,128]{2,1,0:T(8,128)S(1)} %get-tuple-element.400), channel_id=1, source_target_pairs={{2,0},{3,1},{4,2},{5,3},{6,4},{7,5}} | collective-permute-start | bytes 1572872 | tf_op jit(solution)/shard_map/ppermute | solution.py:71
  132.4 1.9 %collective-permute-start.5 = (f32[2,512,128]{2,1,0:T(8,128)S(1)}, f32[2,512,128]{2,1,0:T(8,128)S(1)}, u32[]{:S(2)}, u32[]{:S(2)}) collective-permute-start(f32[2,512,128]{2,1,0:T(8,128)S(1)} %get-tuple-element.399), channel_id=1, source_target_pairs={{3,0},{4,1},{5,2},{6,3},{7,4}} | collective-permute-start | bytes 1572872 | tf_op jit(solution)/shard_map/ppermute | solution.py:71
  134.3 7.8 %collective-permute-done.3 = f32[2,512,128]{2,1,0:T(8,128)S(1)} collective-permute-done((f32[2,512,128]{2,1,0:T(8,128)S(1)}, f32[2,512,128]{2,1,0:T(8,128)S(1)}, u32[]{:S(2)}, u32[]{:S(2)}) %collective-permute-start.3) | collective-permute-done | bytes 524320 | tf_op jit(solution)/shard_map/ppermute | solution.py:71
  142.0 3.8 %collective-permute-done.4 = f32[2,512,128]{2,1,0:T(8,128)S(1)} collective-permute-done((f32[2,512,128]{2,1,0:T(8,128)S(1)}, f32[2,512,128]{2,1,0:T(8,128)S(1)}, u32[]{:S(2)}, u32[]{:S(2)}) %collective-permute-start.4) | collective-permute-done | bytes 524320 | tf_op jit(solution)/shard_map/ppermute | solution.py:71
  145.8 14.8 %collective-permute-done.5 = f32[2,512,128]{2,1,0:T(8,128)S(1)} collective-permute-done((f32[2,512,128]{2,1,0:T(8,128)S(1)}, f32[2,512,128]{2,1,0:T(8,128)S(1)}, u32[]{:S(2)}, u32[]{:S(2)}) %collective-permute-start.5) | collective-permute-done | bytes 524320 | tf_op jit(solution)/shard_map/ppermute | solution.py:71
  (185 shorter events, 48.2 us)
Async XLA Ops:
  0.6 81.9 %copy-start.7 = (bf16[512,2,128]{2,1,0:T(2,128)(2,1)S(1)}, bf16[512,2,128]{2,1,0:T(2,128)(2,1)}, u32[]{:S(2)}) copy-start(bf16[512,2,128]{2,1,0:T(2,128)(2,1)} %param.16) | copy-start | bytes 786436
  0.6 81.9 %copy-start.4 = (bf16[512,2,128]{2,1,0:T(2,128)(2,1)S(1)}, bf16[512,2,128]{2,1,0:T(2,128)(2,1)}, u32[]{:S(2)}) copy-start(bf16[512,2,128]{2,1,0:T(2,128)(2,1)} %param.18) | copy-start | bytes 786436
  1.7 81.9 %collective-permute-start = (bf16[2,512,128]{2,1,0:T(8,128)(2,1)S(1)}, bf16[2,512,128]{2,1,0:T(8,128)(2,1)S(1)}, u32[]{:S(2)}, u32[]{:S(2)}) collective-permute-start(bf16[2,512,128]{2,1,0:T(8,128)(2,1)S(1)} %pad_maximum_fusion.1), channel_id=1, source_target_pairs={{0,3},{1,4},{2,5},{3,6},{4,7}} | collective-permute-start | bytes 786440 | tf_op jit(solution)/shard_map/ppermute | solution.py:59
  5.4 78.2 %collective-permute-start.1 = (bf16[2,512,128]{2,1,0:T(8,128)(2,1)S(1)}, bf16[2,512,128]{2,1,0:T(8,128)(2,1)S(1)}, u32[]{:S(2)}, u32[]{:S(2)}) collective-permute-start(bf16[2,512,128]{2,1,0:T(8,128)(2,1)S(1)} %pad_maximum_fusion.1), channel_id=1, source_target_pairs={{0,2},{1,3},{2,4},{3,5},{4,6},{5,7}} | collective-permute-start | bytes 786440 | tf_op jit(solution)/shard_map/ppermute | solution.py:59
  7.3 76.2 %collective-permute-start.2 = (bf16[2,512,128]{2,1,0:T(8,128)(2,1)S(1)}, bf16[2,512,128]{2,1,0:T(8,128)(2,1)S(1)}, u32[]{:S(2)}, u32[]{:S(2)}) collective-permute-start(bf16[2,512,128]{2,1,0:T(8,128)(2,1)S(1)} %pad_maximum_fusion.1), channel_id=1, source_target_pairs={{0,1},{1,2},{2,3},{3,4},{4,5},{5,6},{6,7}} | collective-permute-start | bytes 786440 | tf_op jit(solution)/shard_map/ppermute | solution.py:59
  10.9 72.5 %copy-start.8 = (f32[512,2]{0,1:T(2,128)S(1)}, f32[512,2]{0,1:T(2,128)}, u32[]{:S(2)}) copy-start(f32[512,2]{0,1:T(2,128)} %param.17) | copy-start | bytes 12292
  10.9 72.7 %copy-start.5 = (bf16[512,128]{1,0:T(8,128)(2,1)S(1)}, bf16[512,128]{1,0:T(8,128)(2,1)}, u32[]{:S(2)}) copy-start(bf16[512,128]{1,0:T(8,128)(2,1)} %param.15) | copy-start | bytes 393220
  11.0 72.7 %copy-start.6 = (bf16[512,128]{1,0:T(8,128)(2,1)S(1)}, bf16[512,128]{1,0:T(8,128)(2,1)}, u32[]{:S(2)}) copy-start(bf16[512,128]{1,0:T(8,128)(2,1)} %param.14) | copy-start | bytes 393220
  84.6 1.4 copy-start.3
  86.4 1.2 copy-start
  89.7 1.4 copy-start.3
  91.5 1.2 copy-start
  94.8 1.4 copy-start.3
  96.6 1.2 copy-start
  99.9 1.4 copy-start.3
  101.7 1.2 copy-start
  105.0 1.4 copy-start.3
  110.1 1.4 copy-start.3
  115.3 1.4 copy-start.3
  120.4 1.4 copy-start.3
  125.5 35.2 %copy-start.2 = (f32[2048,128]{1,0:T(8,128)S(1)}, f32[2048,128]{1,0:T(8,128)}, u32[]{:S(2)}) copy-start(f32[2048,128]{1,0:T(8,128)} %get-tuple-element.211) | copy-start | bytes 3145732
  126.8 15.3 %collective-permute-start.3 = (f32[2,512,128]{2,1,0:T(8,128)S(1)}, f32[2,512,128]{2,1,0:T(8,128)S(1)}, u32[]{:S(2)}, u32[]{:S(2)}) collective-permute-start(f32[2,512,128]{2,1,0:T(8,128)S(1)} %get-tuple-element.398), channel_id=1, source_target_pairs={{1,0},{2,1},{3,2},{4,3},{5,4},{6,5},{7,6}} | collective-permute-start | bytes 1572872 | tf_op jit(solution)/shard_map/ppermute | solution.py:71
  129.1 16.8 %collective-permute-start.4 = (f32[2,512,128]{2,1,0:T(8,128)S(1)}, f32[2,512,128]{2,1,0:T(8,128)S(1)}, u32[]{:S(2)}, u32[]{:S(2)}) collective-permute-start(f32[2,512,128]{2,1,0:T(8,128)S(1)} %get-tuple-element.400), channel_id=1, source_target_pairs={{2,0},{3,1},{4,2},{5,3},{6,4},{7,5}} | collective-permute-start | bytes 1572872 | tf_op jit(solution)/shard_map/ppermute | solution.py:71
  132.4 28.3 %collective-permute-start.5 = (f32[2,512,128]{2,1,0:T(8,128)S(1)}, f32[2,512,128]{2,1,0:T(8,128)S(1)}, u32[]{:S(2)}, u32[]{:S(2)}) collective-permute-start(f32[2,512,128]{2,1,0:T(8,128)S(1)} %get-tuple-element.399), channel_id=1, source_target_pairs={{3,0},{4,1},{5,2},{6,3},{7,4}} | collective-permute-start | bytes 1572872 | tf_op jit(solution)/shard_map/ppermute | solution.py:71
  (12 other events, 12.9 us)
where the time goes:
time: 164 us; the launch traced here: 162 us
  other arithmetic  71 us (43%)
  local copies, waits for them, and re-layouts  31.7 us (19%)
  waiting for transfers between devices  26.4 us (16%)
  starting transfers between devices  15.9 us (10%)
  matrix products  15.2 us (9%)
    select_n x8, other arithmetic, doc_ids(): jnp.searchsorted(bounds[1:], positions, side='right').astype(jnp.int32)  65.7 us
    ppermute x3, waiting for transfers between devices, local(): lax.ppermute(part_sums[:, HOPS - hop], seq_axes, [(sender, sender - hop)...  26.4 us
    while x48, local copies, waits for them, and re-layouts  11.5 us
    ppermute x3, starting transfers between devices, local(): lax.ppermute(kv_pair, seq_axes, [(sender, sender + hop) for sender in ran...  8.44 us
    ppermute x3, starting transfers between devices, local(): lax.ppermute(part_sums[:, HOPS - hop], seq_axes, [(sender, sender - hop)...  7.48 us
    dynamic_slice x16, local copies, waits for them, and re-layouts, window_backward(): (dk_sum, dv_sum), dq_blocks = lax.scan(step, init, blocks)  6.58 us
    gather x8, local copies, waits for them, and re-layouts, doc_ids(): jnp.searchsorted(bounds[1:], positions, side='right').astype(jnp.int32)  5.7 us
    dynamic_update_slice x8, local copies, waits for them, and re-layouts, window_backward(): (dk_sum, dv_sum), dq_blocks = lax.scan(step, init, blocks)  5.19 us
  transfers between devices with their start and end apart: 6, of which 3 were waited for; matrix products, arithmetic and copies ran while one was open for 45% of the time, Pallas kernels for 0%

commit v1 on v0

v1 whole, which is shorter than its diff:
```python
import functools
import math

import jax
import jax.numpy as jnp
from jax import lax
from jax.experimental import pallas as pl
from jax.experimental.pallas import tpu as pltpu
from jax.sharding import PartitionSpec as P

MESH = pl.DeviceIdType.MESH
HOPS = 3
NK = 2
NQ = 4
NONE = 31
NOBODY = 63
FINISH = 18

KV_OWN = {0: [(1, 1), (2, 2)], 1: [(3, 2), (4, 3)], 2: [(3, 1), (0, 1)], 3: [(6, 3)], 4: [(5, 1), (6, 2)], 5: [(7, 2)], 6: [(7, 1)], 7: []}
QD_OWN = {0: [], 1: [(0, 1)], 2: [(0, 2)], 3: [(2, 1), (1, 2)], 4: [(1, 3)], 5: [(4, 1), (7, 1)], 6: [(4, 2), (3, 3)], 7: [(6, 1), (5, 2)]}
KV_REL = {(0, 1): (4, 2), (2, 2): (3, 3), (3, 2): (2, 1), (4, 2): (5, 3), (4, 1): (5, 2), (6, 3): (4, 1), (6, 2): (7, 3), (7, 2): (6, 1)}
QD_REL = {(0, 2): (1, 1), (1, 2): (0, 3), (1, 3): (3, 1), (3, 1): (2, 2), (3, 2): (2, 3), (4, 2): (5, 1), (5, 2): (4, 3), (7, 1): (3, 2)}
ORDER = {
    0: "Q1.0 Q1.1 Q1.2 Q1.3 K1.0 Q3.0 K1.1 Q3.1 Q2.0 Q3.2 Q2.1 Q3.3 Q2.2 Q2.3",
    1: "K1.0 K1.1 F Q3.0 Q2.0 Q3.1 Q3.2 Q2.1 Q3.3 Q2.2 Q1.0 Q2.3 Q1.1 Q1.2 Q1.3",
    2: "Q1.0 Q1.1 Q1.2 Q1.3 K2.0 K1.0 K2.1 K1.1 F Q2.0 Q2.1 Q2.2 Q3.0 Q2.3 Q3.1 Q3.2 Q3.3",
    3: "K1.0 K1.1 Q3.0 K2.0 Q3.1 K3.0 Q3.2 K2.1 Q3.3 K3.1 F Q1.0 Q1.1 Q1.2 Q2.0 Q1.3 Q2.1 Q2.2 Q2.3",
    4: "Q1.0 Q1.1 Q1.2 Q1.3 K3.0 Q2.0 K3.1 Q3.0 Q2.1 K2.0 Q3.1 Q2.2 K2.1 Q3.2 Q2.3 Q3.3 K1.0 K1.1 F",
    5: "K1.0 K1.1 Q2.0 Q1.0 Q2.1 Q1.1 K3.0 Q2.2 Q1.2 K3.1 Q2.3 Q1.3 K2.0 K2.1 F",
    6: "Q1.0 Q1.1 Q1.2 Q1.3 K3.0 K2.0 K3.1 K1.0 K2.1 K1.1 F",
    7: "K1.0 K1.1 K2.0 K3.0 K2.1 K3.1 F Q1.0 Q1.1 Q1.2 Q1.3",
}


def step_codes(text):
    codes = []
    for word in text.split():
        if word == "F":
            codes.append(FINISH)
            continue
        hop, chunk = int(word[1]) - 1, int(word[3])
        codes.append(hop * NK + chunk if word[0] == "K" else 3 * NK + hop * NQ + chunk)
    return codes


def targets_of(table, pick):
    pairs = [table.get(pick(d), NOBODY) for d in range(8)]
    return [p if p == NOBODY else p[0] * 4 + p[1] for p in pairs]


def nth(table, n):
    return [NOBODY if len(table[d]) <= n else table[d][n][0] * 4 + table[d][n][1] for d in range(8)]


def partners():
    near = {d: set() for d in range(8)}
    for table in (KV_OWN, QD_OWN):
        for d, pairs in table.items():
            for target, _ in pairs:
                near[d].add(target)
                near[target].add(d)
    for table in (KV_REL, QD_REL):
        for (d, _), (target, _) in table.items():
            near[d].add(target)
            near[target].add(d)
    return near


def body(
    cu_ref, q_hbm, k_hbm, v_hbm, o_hbm, lse_hbm, do_hbm,
    dq_out, dk_out, dv_out,
    q_loc, k_loc, v_loc, o_loc, lse_loc, do_loc, stat_loc, starts,
    k_buf, v_buf, q_buf, do_buf, stat_buf,
    dqt, dk_acc, dv_acc, dq_st, dk_st, dv_st,
    in_sem, out_sem,
    k_recv, v_recv, q_recv, do_recv, stat_recv,
    k_own, v_own, q_own, do_own, stat_own,
    k_rel, v_rel, q_rel, do_rel, stat_rel,
):
    rows = k_loc.shape[0]
    qrows = q_loc.shape[0]
    head = k_loc.shape[1]
    kc_rows = rows // NK
    qc_rows = qrows // NQ
    scale = head ** -0.5
    factor = scale * math.log2(math.e)
    me = lax.axis_index("cpo") * 4 + lax.axis_index("cp")

    def lut(values):
        out = jnp.int32(values[0])
        for d in range(1, len(values)):
            out = jnp.where(me == d, jnp.int32(values[d]), out)
        return out

    def place(target):
        return {"cpo": target // 4, "cp": target % 4}

    loads = [
        pltpu.make_async_copy(src, dst, in_sem.at[i])
        for i, (src, dst) in enumerate(
            [(k_hbm, k_loc), (v_hbm, v_loc), (q_hbm, q_loc), (do_hbm, do_loc), (o_hbm, o_loc), (lse_hbm, lse_loc)]
        )
    ]
    for load in loads:
        load.start()

    barrier = pltpu.get_barrier_semaphore()
    near = partners()
    for d in range(8):
        @pl.when(me == d)
        def _(d=d):
            for other in sorted(near[d]):
                pl.semaphore_signal(barrier, inc=1, device_id=place(other), device_id_type=MESH)
    lane = lax.broadcasted_iota(jnp.int32, (1, qrows), 1) // 2
    for h in range(HOPS + 1):
        pos = lane + (me + h) * rows
        start = jnp.zeros_like(pos)
        for j in range(cu_ref.shape[0]):
            start = jnp.maximum(start, jnp.where(pos >= cu_ref[j], cu_ref[j], 0))
        starts[h] = start
    for d in range(8):
        @pl.when(me == d)
        def _(d=d):
            pl.semaphore_wait(barrier, len(near[d]))

    def kv_copies(src_k, src_v, sems_k, sems_v, code, slot, chunk):
        target, there = code // 4, code % 4 - 1
        part = pl.ds(chunk * kc_rows, kc_rows)
        return [
            pltpu.make_async_remote_copy(
                src_ref=src.at[part], dst_ref=buf.at[there, part], send_sem=sems.at[slot, chunk], recv_sem=recv.at[there, chunk],
                device_id=place(target), device_id_type=MESH)
            for src, buf, sems, recv in ((src_k, k_buf, sems_k, k_recv), (src_v, v_buf, sems_v, v_recv))
        ]

    def qd_copies(src_q, src_do, sems_q, sems_do, code, slot, chunk):
        target, there = code // 4, code % 4 - 1
        part = pl.ds(chunk * qc_rows, qc_rows)
        return [
            pltpu.make_async_remote_copy(
                src_ref=src.at[part], dst_ref=buf.at[there, part], send_sem=sems.at[slot, chunk], recv_sem=recv.at[there, chunk],
                device_id=place(target), device_id_type=MESH)
            for src, buf, sems, recv in ((src_q, q_buf, sems_q, q_recv), (src_do, do_buf, sems_do, do_recv))
        ]

    def stat_copy(src, sems, code, slot):
        target, there = code // 4, code % 4 - 1
        return pltpu.make_async_remote_copy(
            src_ref=src, dst_ref=stat_buf.at[there], send_sem=sems.at[slot], recv_sem=stat_recv.at[there],
            device_id=place(target), device_id_type=MESH)

    kv_to = [lut(nth(KV_OWN, n)) for n in range(2)]
    qd_to = [lut(nth(QD_OWN, n)) for n in range(2)]

    loads[0].wait()
    loads[1].wait()
    for chunk in range(NK):
        for n in range(2):
            @pl.when(kv_to[n] != NOBODY)
            def _(n=n, chunk=chunk):
                for copy in kv_copies(k_loc, v_loc, k_own, v_own, kv_to[n], n, chunk):
                    copy.start()
    loads[2].wait()
    loads[3].wait()

    def send_qd(chunk):
        for n in range(2):
            @pl.when(qd_to[n] != NOBODY)
            def _(n=n):
                for copy in qd_copies(q_loc, do_loc, q_own, do_own, qd_to[n], n, chunk):
                    copy.start()

    send_qd(0)
    loads[4].wait()
    loads[5].wait()

    wide = lax.broadcasted_iota(jnp.int32, (2, 128), 1)
    for j in range(qrows // 128):
        src = lse_loc[:, 128 * (j // 2):128 * (j // 2 + 1)]
        both = jnp.take_along_axis(src, 64 * (j % 2) + wide // 2, axis=1, mode="promise_in_bounds")
        row = jnp.where(wide[0:1] % 2 == 0, both[0:1], both[1:2])
        stat_loc[0:1, 128 * j:128 * (j + 1)] = row * math.log2(math.e)
    ones = jnp.ones((8, head), jnp.bfloat16)
    for j in range(qrows // 256):
        part = pl.ds(256 * j, 256)
        prod = do_loc[part].astype(jnp.float32) * o_loc[part].astype(jnp.float32)
        hi = prod.astype(jnp.bfloat16)
        lo = (prod - hi.astype(jnp.float32)).astype(jnp.bfloat16)
        dims = (((1,), (1,)), ((), ()))
        total = lax.dot_general(ones, hi, dims, preferred_element_type=jnp.float32)
        total = total + lax.dot_general(ones, lo, dims, preferred_element_type=jnp.float32)
        stat_loc[1:2, 256 * j:256 * (j + 1)] = total[0:1]
    for n in range(2):
        @pl.when(qd_to[n] != NOBODY)
        def _(n=n):
            stat_copy(stat_loc, stat_own, qd_to[n], n).start()
    for chunk in range(1, NQ):
        send_qd(chunk)

    def block(k_blk, v_blk, q_blk, do_blk, lse_row, d_row, keep):
        dims = (((1,), (1,)), ((), ()))
        scores = lax.dot_general(k_blk, q_blk, dims, preferred_element_type=jnp.float32)
        p_mat = jnp.where(keep, jnp.exp2(scores * factor - lse_row), 0.0)
        dp_mat = lax.dot_general(v_blk, do_blk, dims, preferred_element_type=jnp.float32)
        ds_mat = (p_mat * (dp_mat - d_row)).astype(jnp.bfloat16)
        return p_mat.astype(jnp.bfloat16), ds_mat

    def dq_term(k_blk, ds_mat):
        return lax.dot_general(k_blk, ds_mat, (((0,), (0,)), ((), ())), preferred_element_type=jnp.float32)

    kb_rows = 256
    qb_rows = 256
    key_iota = lax.broadcasted_iota(jnp.int32, (kb_rows, qb_rows), 0)
    tok_iota = lax.broadcasted_iota(jnp.int32, (kb_rows, qb_rows), 1) // 2

    for qb in range(qrows // qb_rows):
        cols = pl.ds(qb * qb_rows, qb_rows)
        q_blk, do_blk = q_loc[cols], do_loc[cols]
        dq_sum = None
        for kb in range((qb * qb_rows // 2) // kb_rows + 1):
            keys = pl.ds(kb * kb_rows, kb_rows)
            k_blk = k_loc[keys]
            key_pos = key_iota + (me * rows + kb * kb_rows)
            keep = key_pos >= starts[0, :, cols]
            if kb == (qb * qb_rows // 2) // kb_rows:
                keep = keep & (key_iota + kb * kb_rows <= tok_iota + qb * qb_rows // 2)
            p_low, ds_mat = block(k_blk, v_loc[keys], q_blk, do_blk, stat_loc[0:1, cols], stat_loc[1:2, cols], keep)
            term = dq_term(k_blk, ds_mat)
            dq_sum = term if dq_sum is None else dq_sum + term
            dv_new = jnp.dot(p_low, do_blk, preferred_element_type=jnp.float32)
            dk_new = jnp.dot(ds_mat, q_blk, preferred_element_type=jnp.float32)
            if qb == 0 or kb * kb_rows == qb * qb_rows // 2:
                dv_acc[keys] = dv_new
                dk_acc[keys] = dk_new
            else:
                dv_acc[keys] = dv_acc[keys] + dv_new
                dk_acc[keys] = dk_acc[keys] + dk_new
        dqt[:, cols] = dq_sum

    def kv_unit(slot, chunk):
        keys = pl.ds(chunk * kc_rows, kc_rows)
        k_blk = k_buf[slot, keys]
        v_blk = v_buf[slot, keys]
        base = (me - 1 - slot) * rows + chunk * kc_rows
        for qb in range(qrows // qb_rows):
            cols = pl.ds(qb * qb_rows, qb_rows)
            keep = key_iota >= starts[0, :, cols] - base
            _, ds_mat = block(k_blk, v_blk, q_loc[cols], do_loc[cols], stat_loc[0:1, cols], stat_loc[1:2, cols], keep)
            dqt[:, cols] = dqt[:, cols] + dq_term(k_blk, ds_mat)

    def qd_unit(slot, chunk):
        part = pl.ds(chunk * qc_rows, qc_rows)
        cols = pl.ds(pl.multiple_of(chunk * qc_rows, 128), qc_rows)
        q_blk = q_buf[slot, part]
        do_blk = do_buf[slot, part]
        lse_row = stat_buf[slot, 0:1, cols]
        d_row = stat_buf[slot, 1:2, cols]
        start = starts[slot + 1, :, cols] - me * rows
        for kb in range(rows // kb_rows):
            keys = pl.ds(kb * kb_rows, kb_rows)
            keep = key_iota >= start - kb * kb_rows
            p_low, ds_mat = block(k_loc[keys], v_loc[keys], q_blk, do_blk, lse_row, d_row, keep)
            dv_acc[keys] = dv_acc[keys] + jnp.dot(p_low, do_blk, preferred_element_type=jnp.float32)
            dk_acc[keys] = dk_acc[keys] + jnp.dot(ds_mat, q_blk, preferred_element_type=jnp.float32)

    kv_on = [lut(targets_of(KV_REL, lambda d, h=h: (d, h + 1))) for h in range(HOPS)]
    qd_on = [lut(targets_of(QD_REL, lambda d, h=h: (d, h + 1))) for h in range(HOPS)]

    def pick(values, slot):
        return jnp.where(slot == 0, values[0], jnp.where(slot == 1, values[1], values[2]))

    per_word = 6
    codes = {d: step_codes(ORDER[d]) for d in range(8)}
    steps = max(len(c) for c in codes.values())
    words = -(-steps // per_word)
    packed = []
    for w in range(words):
        values = []
        for d in range(8):
            part = (codes[d] + [NONE] * (words * per_word))[w * per_word:(w + 1) * per_word]
            values.append(sum(c * 32 ** i for i, c in enumerate(part)))
        packed.append(lut(values))

    def step(i, carry):
        code = carry[0] % 32

        @pl.when(code < 3 * NK)
        def _():
            slot, chunk = code // NK, code % NK
            to = pick(kv_on, slot)
            for copy in kv_copies(k_buf.at[slot], v_buf.at[slot], k_rel, v_rel, me * 4 + slot + 1, slot, chunk):
                copy.wait_recv()

            @pl.when(to != NOBODY)
            def _():
                for copy in kv_copies(k_buf.at[slot], v_buf.at[slot], k_rel, v_rel, to, slot, chunk):
                    copy.start()

            @pl.when(me > slot)
            def _():
                kv_unit(slot, chunk)

        @pl.when((code >= 3 * NK) & (code < FINISH))
        def _():
            slot, chunk = (code - 3 * NK) // NQ, (code - 3 * NK) % NQ
            to = pick(qd_on, slot)
            for copy in qd_copies(q_buf.at[slot], do_buf.at[slot], q_rel, do_rel, me * 4 + slot + 1, slot, chunk):
                copy.wait_recv()

            @pl.when(to != NOBODY)
            def _():
                for copy in qd_copies(q_buf.at[slot], do_buf.at[slot], q_rel, do_rel, to, slot, chunk):
                    copy.start()

            @pl.when(chunk == 0)
            def _():
                stat_copy(stat_buf.at[slot], stat_rel, me * 4 + slot + 1, slot).wait_recv()

                @pl.when(to != NOBODY)
                def _():
                    stat_copy(stat_buf.at[slot], stat_rel, to, slot).start()

            @pl.when(me + slot < 7)
            def _():
                qd_unit(slot, chunk)

        last = (i % per_word) == per_word - 1
        rest = [jnp.where(last, (carry + (jnp.int32(0),))[w + 1], carry[w] // 32 if w == 0 else carry[w]) for w in range(words)]
        return tuple(rest)

    lax.fori_loop(0, steps, step, tuple(packed))

    dq_st[...] = (jnp.transpose(dqt[...]) * scale).astype(jnp.bfloat16)
    dk_st[...] = (dk_acc[...] * scale).astype(jnp.bfloat16)
    dv_st[...] = dv_acc[...].astype(jnp.bfloat16)
    stores = [
        pltpu.make_async_copy(src, dst, out_sem.at[i])
        for i, (src, dst) in enumerate([(dq_st, dq_out), (dk_st, dk_out), (dv_st, dv_out)])
    ]
    for store in stores:
        store.start()

    for chunk in range(NK):
        for n in range(2):
            @pl.when(kv_to[n] != NOBODY)
            def _(n=n, chunk=chunk):
                for copy in kv_copies(k_loc, v_loc, k_own, v_own, kv_to[n], n, chunk):
                    copy.wait_send()
        for h in range(HOPS):
            @pl.when(kv_on[h] != NOBODY)
            def _(h=h, chunk=chunk):
                for copy in kv_copies(k_buf.at[h], v_buf.at[h], k_rel, v_rel, kv_on[h], h, chunk):
                    copy.wait_send()
    for n in range(2):
        @pl.when(qd_to[n] != NOBODY)
        def _(n=n):
            stat_copy(stat_loc, stat_own, qd_to[n], n).wait_send()
            for chunk in range(NQ):
                for copy in qd_copies(q_loc, do_loc, q_own, do_own, qd_to[n], n, chunk):
                    copy.wait_send()
    for h in range(HOPS):
        @pl.when(qd_on[h] != NOBODY)
        def _(h=h):
            stat_copy(stat_buf.at[h], stat_rel, qd_on[h], h).wait_send()
            for chunk in range(NQ):
                for copy in qd_copies(q_buf.at[h], do_buf.at[h], q_rel, do_rel, qd_on[h], h, chunk):
                    copy.wait_send()
    for store in stores:
        store.wait()


def solution(mesh):
    def local(queries, keys, values, attn_out, logsumexp, d_out, cu_seqlens):
        rows, heads, head = queries.shape
        qrows = rows * heads
        bf, f32 = jnp.bfloat16, jnp.float32
        dma = pltpu.SemaphoreType.DMA
        any_spec = pl.BlockSpec(memory_space=pl.ANY)
        d_query, d_key, d_value = pl.pallas_call(
            body,
            name="packed_backward",
            out_shape=(
                jax.ShapeDtypeStruct((qrows, head), bf),
                jax.ShapeDtypeStruct((rows, head), bf),
                jax.ShapeDtypeStruct((rows, head), bf),
            ),
            in_specs=[pl.BlockSpec(memory_space=pltpu.SMEM)] + [any_spec] * 6,
            out_specs=(any_spec,) * 3,
            scratch_shapes=[
                pltpu.VMEM((qrows, head), bf), pltpu.VMEM((rows, head), bf), pltpu.VMEM((rows, head), bf),
                pltpu.VMEM((qrows, head), bf), pltpu.VMEM((heads, rows), f32), pltpu.VMEM((qrows, head), bf),
                pltpu.VMEM((2, qrows), f32), pltpu.VMEM((HOPS + 1, 1, qrows), jnp.int32),
                pltpu.VMEM((HOPS, rows, head), bf), pltpu.VMEM((HOPS, rows, head), bf),
                pltpu.VMEM((HOPS, qrows, head), bf), pltpu.VMEM((HOPS, qrows, head), bf), pltpu.VMEM((HOPS, 2, qrows), f32),
                pltpu.VMEM((head, qrows), f32), pltpu.VMEM((rows, head), f32), pltpu.VMEM((rows, head), f32),
                pltpu.VMEM((qrows, head), bf), pltpu.VMEM((rows, head), bf), pltpu.VMEM((rows, head), bf),
                dma((6,)), dma((3,)),
                dma((HOPS, NK)), dma((HOPS, NK)), dma((HOPS, NQ)), dma((HOPS, NQ)), dma((HOPS,)),
                dma((2, NK)), dma((2, NK)), dma((2, NQ)), dma((2, NQ)), dma((2,)),
                dma((HOPS, NK)), dma((HOPS, NK)), dma((HOPS, NQ)), dma((HOPS, NQ)), dma((HOPS,)),
            ],
            compiler_params=pltpu.CompilerParams(collective_id=0, has_side_effects=True),
        )(cu_seqlens, queries.reshape(qrows, head), keys, values, attn_out.reshape(qrows, head), logsumexp.T, d_out.reshape(qrows, head))
        return d_query.reshape(rows, heads, head), d_key, d_value

    seq_spec = P(("dp", "cpo", "cp"))
    return jax.shard_map(local, mesh=mesh, in_specs=(seq_spec,) * 6 + (P("dp"),), out_specs=(seq_spec,) * 3, check_vma=False)
```

time: 164 us -> 29.4 us (0.18)
  the two profiles are of different devices: /device:TPU:3 before, /device:TPU:2 now
where the time goes in v1:
time: 29.4 us; the launch traced here: 29.2 us
  Pallas kernels  25.1 us (85%)
  local copies, waits for them, and re-layouts  3.48 us (12%)
  between operations  0.65 us (2%)
    pallas_call x1, Pallas kernels, local(): pl.pallas_call(body, name='packed_backward', out_shape=(jax.ShapeDtypeStr...  25.1 us
    unnamed x7, local copies, waits for them, and re-layouts  3.48 us

profile of v1, /device:TPU:2, one launch (start us, length us, event | category | flops | bytes accessed | tf_op | source)
XLA Modules:
  0.0 29.2 jit_solution(2618798111984678231)
XLA Ops:
  0.6 25.1 %packed_backward.1 = (bf16[1024,128]{1,0:T(8,128)(2,1)}, bf16[512,128]{1,0:T(8,128)(2,1)}, bf16[512,128]{1,0:T(8,128)(2,1)}) custom-call(s32[14]{0:T(128)} %cu_ref.1, bf16[1024,128]{1,0:T(8,128)(2,1)} %bitcast.6, bf16[512,128]{1,0:T(8,128)(2,1)} %k_hbm.1, bf16[512,128]{1,0:T(8,128)(2,1)} %v_hbm.1, bf16[1024,128]{1,0:T(8,128)(2,1)} %bitcast.7, ...), custom_call_target="tpu_custom_call" | custom-call | tf_op jit(solution)/shard_map/packed_backward/pallas_call | solution.py:379
  25.7 0.0 copy-start.1
  25.8 1.9 %copy.13 = bf16[512,2,128]{2,1,0:T(2,128)(2,1)} copy(bf16[512,2,128]{2,1,0:T(2,128)(2,1)} %bitcast.5) | data formatting | bytes 524288
  27.6 0.0 copy-done.1
  27.6 0.0 copy-start
  27.6 0.7 %copy.14 = bf16[512,128]{1,0:T(8,128)(2,1)} copy(bf16[512,128]{1,0:T(8,128)(2,1)S(1)} %copy-done.1) | data formatting | bytes 262144
  28.3 0.3 %copy-done = bf16[512,128]{1,0:T(8,128)(2,1)S(1)} copy-done((bf16[512,128]{1,0:T(8,128)(2,1)S(1)}, bf16[512,128]{1,0:T(8,128)(2,1)}, u32[]{:S(2)}) %copy-start) | copy-done | bytes 131096
  28.6 0.7 %copy.15 = bf16[512,128]{1,0:T(8,128)(2,1)} copy(bf16[512,128]{1,0:T(8,128)(2,1)S(1)} %copy-done) | data formatting | bytes 262144
Async XLA Ops:
  25.7 1.9 %copy-start.1 = (bf16[512,128]{1,0:T(8,128)(2,1)S(1)}, bf16[512,128]{1,0:T(8,128)(2,1)}, u32[]{:S(2)}) copy-start(bf16[512,128]{1,0:T(8,128)(2,1)} %get-tuple-element.13) | copy-start | bytes 393220
  27.6 1.0 %copy-start = (bf16[512,128]{1,0:T(8,128)(2,1)S(1)}, bf16[512,128]{1,0:T(8,128)(2,1)}, u32[]{:S(2)}) copy-start(bf16[512,128]{1,0:T(8,128)(2,1)} %get-tuple-element.14) | copy-start | bytes 393220

commit v2 on v1

v2 whole, which is shorter than its diff:
```python
import functools
import math

import jax
import jax.numpy as jnp
from jax import lax
from jax.experimental import pallas as pl
from jax.experimental.pallas import tpu as pltpu
from jax.sharding import PartitionSpec as P

MESH = pl.DeviceIdType.MESH
HOPS = 3
NK = 2
NQ = 4
NONE = 31
NOBODY = 63
SEND = 18

KV_OWN = {0: [(1, 1), (2, 2)], 1: [(3, 2), (4, 3)], 2: [(3, 1), (4, 2)], 3: [(6, 3)], 4: [(5, 1), (6, 2)], 5: [(7, 2)], 6: [(7, 1)], 7: []}
QD_OWN = {0: [], 1: [(0, 1)], 2: [(0, 2)], 3: [(2, 1), (1, 2)], 4: [(1, 3)], 5: [(4, 1), (3, 2)], 6: [(4, 2), (3, 3)], 7: [(6, 1), (5, 2)]}
KV_FAR = 2
QD_FAR = 5
FAR_NEWS = ((0, 2, 4), (7, 5, 3))
KV_REL = {(2, 2): (3, 3), (3, 2): (2, 1), (4, 2): (5, 3), (4, 1): (5, 2), (6, 3): (4, 1), (6, 2): (7, 3), (7, 2): (6, 1)}
QD_REL = {(0, 2): (1, 1), (1, 2): (0, 3), (1, 3): (3, 1), (3, 1): (2, 2), (3, 2): (2, 3), (4, 2): (5, 1), (5, 2): (4, 3)}
ORDER = {
    0: (0, 110, 112, 111, 113, 120, 130, 131, 132, 121, 133, 122, 123),
    1: (0, 10, 11, 130, 120, 131, 110, 132, 121, 133, 122, 123, 111, 112, 113),
    2: (0, 110, 112, 111, 113, 20, 10, 21, 11, 120, 130, 121, 122, 131, 132, 123, 133),
    3: (0, 10, 11, 130, 20, 131, 30, 21, 132, 31, 110, 120, 133, 111, 112, 121, 122, 113, 123),
    4: (0, 110, 112, 111, 30, 113, 120, 31, 130, 121, 20, 131, 10, 21, 132, 11, 122, 133, 123),
    5: (0, 10, 11, 120, 110, 121, 111, 30, 122, 20, 31, 123, 21, 112, 113),
    6: (110, 112, 111, 30, 113, 20, 31, 0, 10, 21, 11),
    7: (0, 10, 11, 20, 30, 21, 31),
}


def step_codes(items):
    codes = []
    for item in items:
        if item == 0:
            codes.append(SEND)
            continue
        hop, chunk = item % 100 // 10 - 1, item % 10
        codes.append(hop * NK + chunk if item < 100 else 3 * NK + hop * NQ + chunk)
    return codes


def targets_of(table, pick):
    pairs = [table.get(pick(d), NOBODY) for d in range(8)]
    return [p if p == NOBODY else p[0] * 4 + p[1] for p in pairs]


def nth(table, n):
    return [NOBODY if len(table[d]) <= n else table[d][n][0] * 4 + table[d][n][1] for d in range(8)]


def partners():
    near = {d: set() for d in range(8)}
    for table in (KV_OWN, QD_OWN):
        for d, pairs in table.items():
            for n, (target, _) in enumerate(pairs):
                if n == 1 and d == (KV_FAR if table is KV_OWN else QD_FAR):
                    continue
                near[d].add(target)
                near[target].add(d)
    for messenger, far, target in FAR_NEWS:
        for other in (far, target):
            near[messenger].add(other)
            near[other].add(messenger)
    for table in (KV_REL, QD_REL):
        for (d, _), (target, _) in table.items():
            near[d].add(target)
            near[target].add(d)
    return near


def body(
    cu_ref, q_hbm, k_hbm, v_hbm, o_hbm, lse_hbm, do_hbm,
    dq_out, dk_out, dv_out,
    q_loc, k_loc, v_loc, o_loc, lse_loc, do_loc, stat_loc, starts,
    k_buf, v_buf, q_buf, do_buf, stat_buf,
    dqt, dk_acc, dv_acc, in_sem, far_sem,
    k_recv, v_recv, q_recv, do_recv, stat_recv,
    kv_own, qd_own, stat_own, kv_rel, qd_rel, stat_rel,
):
    rows = k_loc.shape[0]
    qrows = q_loc.shape[0]
    head = k_loc.shape[1]
    kc_rows = rows // NK
    qc_rows = qrows // NQ
    scale = head ** -0.5
    factor = scale * math.log2(math.e)
    me = lax.axis_index("cpo") * 4 + lax.axis_index("cp")

    def lut(values):
        out = jnp.int32(values[0])
        for d in range(1, len(values)):
            out = jnp.where(me == d, jnp.int32(values[d]), out)
        return out

    def place(target):
        return {"cpo": target // 4, "cp": target % 4}

    loads = [
        pltpu.make_async_copy(src, dst, in_sem.at[i])
        for i, (src, dst) in enumerate(
            [(k_hbm, k_loc), (v_hbm, v_loc), (q_hbm, q_loc), (do_hbm, do_loc), (o_hbm, o_loc), (lse_hbm, lse_loc)]
        )
    ]
    for load in loads:
        load.start()

    barrier = pltpu.get_barrier_semaphore()
    near = partners()
    for d in range(8):
        @pl.when(me == d)
        def _(d=d):
            for other in sorted(near[d]):
                pl.semaphore_signal(barrier, inc=1, device_id=place(other), device_id_type=MESH)
    lane = lax.broadcasted_iota(jnp.int32, (1, qrows), 1) // 2
    for h in range(HOPS + 1):
        pos = lane + (me + h) * rows
        start = jnp.zeros_like(pos)
        for j in range(cu_ref.shape[0]):
            start = jnp.maximum(start, jnp.where(pos >= cu_ref[j], cu_ref[j], 0))
        starts[h] = start
    for d in range(8):
        @pl.when(me == d)
        def _(d=d):
            pl.semaphore_wait(barrier, len(near[d]))

    def kv_copies(src_k, src_v, sem, code, chunk):
        target, there = code // 4, code % 4 - 1
        part = pl.ds(chunk * kc_rows, kc_rows)
        return [
            pltpu.make_async_remote_copy(
                src_ref=src.at[part], dst_ref=buf.at[there, part], send_sem=sem, recv_sem=recv.at[there, chunk],
                device_id=place(target), device_id_type=MESH)
            for src, buf, recv in ((src_k, k_buf, k_recv), (src_v, v_buf, v_recv))
        ]

    def qd_copies(src_q, src_do, sem, code, chunk):
        target, there = code // 4, code % 4 - 1
        part = pl.ds(chunk * qc_rows, qc_rows)
        return [
            pltpu.make_async_remote_copy(
                src_ref=src.at[part], dst_ref=buf.at[there, part], send_sem=sem, recv_sem=recv.at[there, chunk],
                device_id=place(target), device_id_type=MESH)
            for src, buf, recv in ((src_q, q_buf, q_recv), (src_do, do_buf, do_recv))
        ]

    def stat_copy(src, sem, code):
        target, there = code // 4, code % 4 - 1
        return pltpu.make_async_remote_copy(
            src_ref=src, dst_ref=stat_buf.at[there], send_sem=sem, recv_sem=stat_recv.at[there],
            device_id=place(target), device_id_type=MESH)

    kv_to = [lut(nth(KV_OWN, n)) for n in range(2)]
    qd_to = [lut(nth(QD_OWN, n)) for n in range(2)]

    def send_kv(n, chunk):
        for copy in kv_copies(k_loc, v_loc, kv_own.at[n], kv_to[n], chunk):
            copy.start()

    def send_qd(n, chunk):
        for copy in qd_copies(q_loc, do_loc, qd_own.at[n], qd_to[n], chunk):
            copy.start()

    kv_near = [kv_to[0] != NOBODY, (kv_to[1] != NOBODY) & (me != KV_FAR)]
    qd_near = [qd_to[0] != NOBODY, (qd_to[1] != NOBODY) & (me != QD_FAR)]
    loads[0].wait()
    loads[1].wait()
    for chunk in range(NK):
        for n in range(2):
            @pl.when(kv_near[n])
            def _(n=n, chunk=chunk):
                send_kv(n, chunk)
    loads[2].wait()
    loads[3].wait()
    for n in range(2):
        @pl.when(qd_near[n])
        def _(n=n):
            send_qd(n, 0)
    for messenger, far, _ in FAR_NEWS:
        @pl.when(me == messenger)
        def _(far=far):
            pl.semaphore_signal(far_sem, inc=1, device_id=place(far), device_id_type=MESH)
    loads[4].wait()
    loads[5].wait()

    wide = lax.broadcasted_iota(jnp.int32, (2, 128), 1)
    for j in range(qrows // 128):
        src = lse_loc[:, 128 * (j // 2):128 * (j // 2 + 1)]
        both = jnp.take_along_axis(src, 64 * (j % 2) + wide // 2, axis=1, mode="promise_in_bounds")
        row = jnp.where(wide[0:1] % 2 == 0, both[0:1], both[1:2])
        stat_loc[0:1, 128 * j:128 * (j + 1)] = row * math.log2(math.e)
    ones = jnp.ones((8, head), jnp.bfloat16)
    for j in range(qrows // 256):
        part = pl.ds(256 * j, 256)
        prod = do_loc[part].astype(jnp.float32) * o_loc[part].astype(jnp.float32)
        hi = prod.astype(jnp.bfloat16)
        lo = (prod - hi.astype(jnp.float32)).astype(jnp.bfloat16)
        dims = (((1,), (1,)), ((), ()))
        total = lax.dot_general(ones, hi, dims, preferred_element_type=jnp.float32)
        total = total + lax.dot_general(ones, lo, dims, preferred_element_type=jnp.float32)
        stat_loc[1:2, 256 * j:256 * (j + 1)] = total[0:1]
    for n in range(2):
        @pl.when(qd_near[n])
        def _(n=n):
            stat_copy(stat_loc, stat_own.at[n], qd_to[n]).start()
            send_qd(n, 1)

    @pl.when(me == KV_FAR)
    def _():
        pl.semaphore_wait(far_sem, 1)
        for chunk in range(NK):
            send_kv(1, chunk)

    @pl.when(me == QD_FAR)
    def _():
        pl.semaphore_wait(far_sem, 1)
        send_qd(1, 0)
        stat_copy(stat_loc, stat_own.at[1], qd_to[1]).start()
        send_qd(1, 1)

    def send_later():
        for chunk in range(2, NQ):
            for n in range(2):
                @pl.when(qd_to[n] != NOBODY)
                def _(n=n, chunk=chunk):
                    send_qd(n, chunk)

    def block(k_blk, v_blk, q_blk, do_blk, lse_row, d_row, keep):
        dims = (((1,), (1,)), ((), ()))
        scores = lax.dot_general(k_blk, q_blk, dims, preferred_element_type=jnp.float32)
        p_mat = jnp.where(keep, jnp.exp2(scores * factor - lse_row), 0.0)
        dp_mat = lax.dot_general(v_blk, do_blk, dims, preferred_element_type=jnp.float32)
        ds_mat = (p_mat * (dp_mat - d_row)).astype(jnp.bfloat16)
        return p_mat.astype(jnp.bfloat16), ds_mat

    def dq_term(k_blk, ds_mat):
        return lax.dot_general(k_blk, ds_mat, (((0,), (0,)), ((), ())), preferred_element_type=jnp.float32)

    def key_iota(keys, width):
        return lax.broadcasted_iota(jnp.int32, (keys, width), 0)

    half = qrows // 2

    def own_half(first, keys):
        cols = pl.ds(first, half)
        q_blk, do_blk, k_blk = q_loc[cols], do_loc[cols], k_loc[0:keys]
        key_pos = key_iota(keys, half)
        tok = lax.broadcasted_iota(jnp.int32, (keys, half), 1) // 2 + first // 2
        keep = (key_pos >= starts[0, :, cols] - me * rows) & (key_pos <= tok)
        p_low, ds_mat = block(k_blk, v_loc[0:keys], q_blk, do_blk, stat_loc[0:1, cols], stat_loc[1:2, cols], keep)
        dqt[:, cols] = dq_term(k_blk, ds_mat)
        dv_new = jnp.dot(p_low, do_blk, preferred_element_type=jnp.float32)
        dk_new = jnp.dot(ds_mat, q_blk, preferred_element_type=jnp.float32)
        if keys == rows:
            dv_acc[...] = dv_new
            dk_acc[...] = dk_new
        else:
            dv_acc[0:keys] = dv_acc[0:keys] + dv_new
            dk_acc[0:keys] = dk_acc[0:keys] + dk_new

    own_half(half, rows)
    own_half(0, rows // 2)

    def kv_unit(slot):
        base = (me - 1 - slot) * rows
        keep = key_iota(rows, qrows) >= starts[0] - base
        k_blk = k_buf[slot]
        _, ds_mat = block(k_blk, v_buf[slot], q_loc[...], do_loc[...], stat_loc[0:1], stat_loc[1:2], keep)
        dqt[...] = dqt[...] + dq_term(k_blk, ds_mat)

    def qd_unit(slot, part):
        cols = pl.ds(pl.multiple_of(part * half, 128), half)
        q_blk = q_buf[slot, cols]
        do_blk = do_buf[slot, cols]
        keep = key_iota(rows, half) >= starts[slot + 1, :, cols] - me * rows
        p_low, ds_mat = block(k_loc[...], v_loc[...], q_blk, do_blk, stat_buf[slot, 0:1, cols], stat_buf[slot, 1:2, cols], keep)
        dv_acc[...] = dv_acc[...] + jnp.dot(p_low, do_blk, preferred_element_type=jnp.float32)
        dk_acc[...] = dk_acc[...] + jnp.dot(ds_mat, q_blk, preferred_element_type=jnp.float32)

    kv_on = [lut(targets_of(KV_REL, lambda d, h=h: (d, h + 1))) for h in range(HOPS)]
    qd_on = [lut(targets_of(QD_REL, lambda d, h=h: (d, h + 1))) for h in range(HOPS)]

    def pick(values, slot):
        return jnp.where(slot == 0, values[0], jnp.where(slot == 1, values[1], values[2]))

    per_word = 6
    codes = {d: step_codes(ORDER[d]) for d in range(8)}
    steps = max(len(c) for c in codes.values())
    words = -(-steps // per_word)
    packed = []
    for w in range(words):
        values = []
        for d in range(8):
            part = (codes[d] + [NONE] * (words * per_word))[w * per_word:(w + 1) * per_word]
            values.append(sum(c * 32 ** i for i, c in enumerate(part)))
        packed.append(lut(values))

    def step(i, carry):
        code = carry[0] % 32

        @pl.when(code < 3 * NK)
        def _():
            slot, chunk = code // NK, code % NK
            to = pick(kv_on, slot)
            for copy in kv_copies(k_buf.at[slot], v_buf.at[slot], kv_rel.at[slot], me * 4 + slot + 1, chunk):
                copy.wait_recv()

            @pl.when(to != NOBODY)
            def _():
                for copy in kv_copies(k_buf.at[slot], v_buf.at[slot], kv_rel.at[slot], to, chunk):
                    copy.start()

            @pl.when((me > slot) & (chunk == NK - 1))
            def _():
                kv_unit(slot)

        @pl.when((code >= 3 * NK) & (code < SEND))
        def _():
            slot, chunk = (code - 3 * NK) // NQ, (code - 3 * NK) % NQ
            to = pick(qd_on, slot)
            for copy in qd_copies(q_buf.at[slot], do_buf.at[slot], qd_rel.at[slot], me * 4 + slot + 1, chunk):
                copy.wait_recv()

            @pl.when(to != NOBODY)
            def _():
                for copy in qd_copies(q_buf.at[slot], do_buf.at[slot], qd_rel.at[slot], to, chunk):
                    copy.start()

            @pl.when(chunk == 0)
            def _():
                stat_copy(stat_buf.at[slot], stat_rel.at[slot], me * 4 + slot + 1).wait_recv()

                @pl.when(to != NOBODY)
                def _():
                    stat_copy(stat_buf.at[slot], stat_rel.at[slot], to).start()

            @pl.when((me + slot < 7) & (chunk % 2 == 1))
            def _():
                qd_unit(slot, chunk // 2)

        @pl.when(code == SEND)
        def _():
            send_later()

        last = (i % per_word) == per_word - 1
        rest = [jnp.where(last, (carry + (jnp.int32(0),))[w + 1], carry[w] // 32 if w == 0 else carry[w]) for w in range(words)]
        return tuple(rest)

    lax.fori_loop(0, steps, step, tuple(packed))

    dq_out[...] = (jnp.transpose(dqt[...]) * scale).astype(jnp.bfloat16)
    dk_out[...] = (dk_acc[...] * scale).astype(jnp.bfloat16)
    dv_out[...] = dv_acc[...].astype(jnp.bfloat16)

    def sent(ref, sem):
        pltpu.make_async_remote_copy(src_ref=ref, dst_ref=ref, send_sem=sem, recv_sem=sem, device_id=place(me), device_id_type=MESH).wait_send()

    for targets, kv_sem in ((kv_to, kv_own), (kv_on, kv_rel)):
        for n, target in enumerate(targets):
            @pl.when(target != NOBODY)
            def _(n=n, kv_sem=kv_sem):
                sent(q_buf.at[0], kv_sem.at[n])
    for targets, qd_sem, stat_sem in ((qd_to, qd_own, stat_own), (qd_on, qd_rel, stat_rel)):
        for n, target in enumerate(targets):
            @pl.when(target != NOBODY)
            def _(n=n, qd_sem=qd_sem, stat_sem=stat_sem):
                sent(q_buf.at[0:2], qd_sem.at[n])
                sent(stat_loc, stat_sem.at[n])


def store_body(dq_ref, dk_ref, dv_ref, dq_out, dk_out, dv_out, sems):
    pairs = ((dq_ref, dq_out), (dk_ref, dk_out), (dv_ref, dv_out))
    copies = [pltpu.make_async_copy(src, dst, sems.at[i]) for i, (src, dst) in enumerate(pairs)]
    for copy in copies:
        copy.start()
    for copy in copies:
        copy.wait()


def solution(mesh):
    def local(queries, keys, values, attn_out, logsumexp, d_out, cu_seqlens):
        rows, heads, head = queries.shape
        qrows = rows * heads
        bf, f32 = jnp.bfloat16, jnp.float32
        dma = pltpu.SemaphoreType.DMA
        any_spec = pl.BlockSpec(memory_space=pl.ANY)
        vmem_spec = pl.BlockSpec(memory_space=pltpu.VMEM)
        shapes = ((qrows, head), (rows, head), (rows, head))
        results = pl.pallas_call(
            body,
            name="packed_backward",
            out_shape=tuple(pltpu.VMEM(shape, bf) for shape in shapes),
            in_specs=[pl.BlockSpec(memory_space=pltpu.SMEM)] + [any_spec] * 6,
            out_specs=(vmem_spec,) * 3,
            scratch_shapes=[
                pltpu.VMEM((qrows, head), bf), pltpu.VMEM((rows, head), bf), pltpu.VMEM((rows, head), bf),
                pltpu.VMEM((qrows, head), bf), pltpu.VMEM((heads, rows), f32), pltpu.VMEM((qrows, head), bf),
                pltpu.VMEM((2, qrows), f32), pltpu.VMEM((HOPS + 1, 1, qrows), jnp.int32),
                pltpu.VMEM((HOPS, rows, head), bf), pltpu.VMEM((HOPS, rows, head), bf),
                pltpu.VMEM((HOPS, qrows, head), bf), pltpu.VMEM((HOPS, qrows, head), bf), pltpu.VMEM((HOPS, 2, qrows), f32),
                pltpu.VMEM((head, qrows), f32), pltpu.VMEM((rows, head), f32), pltpu.VMEM((rows, head), f32),
                dma((6,)), pltpu.SemaphoreType.REGULAR,
                dma((HOPS, NK)), dma((HOPS, NK)), dma((HOPS, NQ)), dma((HOPS, NQ)), dma((HOPS,)),
                dma((2,)), dma((2,)), dma((2,)), dma((HOPS,)), dma((HOPS,)), dma((HOPS,)),
            ],
            compiler_params=pltpu.CompilerParams(collective_id=0, has_side_effects=True),
        )(cu_seqlens, queries.reshape(qrows, head), keys, values, attn_out.reshape(qrows, head), logsumexp.T, d_out.reshape(qrows, head))
        d_query, d_key, d_value = pl.pallas_call(
            store_body,
            name="store",
            out_shape=tuple(jax.ShapeDtypeStruct(shape, bf) for shape in shapes),
            in_specs=[vmem_spec] * 3,
            out_specs=(any_spec,) * 3,
            scratch_shapes=[dma((3,))],
        )(*[pltpu.with_memory_space_constraint(x, pltpu.VMEM) for x in results])
        return d_query.reshape(rows, heads, head), d_key, d_value

    seq_spec = P(("dp", "cpo", "cp"))
    return jax.shard_map(local, mesh=mesh, in_specs=(seq_spec,) * 6 + (P("dp"),), out_specs=(seq_spec,) * 3, check_vma=False)
```

time: 29.4 us -> 26.3 us (0.89)
  local copies, waits for them, and re-layouts: 3.48 us -> 0 us
  Pallas kernels: 25.1 us -> 25.6 us
    unnamed x7 -> x0, local copies, waits for them, and re-layouts: 3.48 us -> none
    pallas_call x1 -> x2, Pallas kernels: 25.1 us -> 25.6 us  [the longest x1 24.8 us: local(): pl.pallas_call(body, name='packed_backward', out_shape=tuple((pltpu.VMEM(...]
where the time goes in v2:
time: 26.3 us; the launch traced here: 26.2 us
  Pallas kernels  25.6 us (97%)
  between operations  0.64 us (2%)
    pallas_call x1, Pallas kernels, local(): pl.pallas_call(body, name='packed_backward', out_shape=tuple((pltpu.VMEM(...  24.8 us
    pallas_call x1, Pallas kernels, local(): pl.pallas_call(store_body, name='store', out_shape=tuple((jax.ShapeDtypeS...  0.81 us

profile of v2, /device:TPU:2, one launch (start us, length us, event | category | flops | bytes accessed | tf_op | source)
XLA Modules:
  0.0 26.2 jit_solution(4208677256637757529)
XLA Ops:
  0.6 24.8 %packed_backward.1 = (bf16[1024,128]{1,0:T(8,128)(2,1)S(1)}, bf16[512,128]{1,0:T(8,128)(2,1)S(1)}, bf16[512,128]{1,0:T(8,128)(2,1)S(1)}) custom-call(s32[14]{0:T(128)} %cu_ref.1, bf16[1024,128]{1,0:T(8,128)(2,1)} %bitcast.5, bf16[512,128]{1,0:T(8,128)(2,1)} %k_hbm.1, bf16[512,128]{1,0:T(8,128)(2,1)} %v_hbm.1, bf16[1024,128]{1,0:T(8,128)(2,1)} %bitcast.6, ...), custom_call_target="tpu_custom_call" | custom-call | tf_op jit(solution)/shard_map/packed_backward/pallas_call | solution.py:395
  25.4 0.8 %store.1 = (bf16[1024,128]{1,0:T(8,128)(2,1)}, bf16[512,128]{1,0:T(8,128)(2,1)}, bf16[512,128]{1,0:T(8,128)(2,1)}) custom-call(bf16[1024,128]{1,0:T(8,128)(2,1)S(1)} %get-tuple-element.9.dq_ref, bf16[512,128]{1,0:T(8,128)(2,1)S(1)} %get-tuple-element.10.dk_ref, bf16[512,128]{1,0:T(8,128)(2,1)S(1)} %get-tuple-element.11.dv_ref), custom_call_target="tpu_custom_call" | custom-call | tf_op jit(solution)/shard_map/store/pallas_call | solution.py:414

commit v3 on v2

--- a/solution.py
+++ b/solution.py
@@ -20,30 +20,37 @@
 QD_OWN = {0: [], 1: [(0, 1)], 2: [(0, 2)], 3: [(2, 1), (1, 2)], 4: [(1, 3)], 5: [(4, 1), (3, 2)], 6: [(4, 2), (3, 3)], 7: [(6, 1), (5, 2)]}
 KV_FAR = 2
 QD_FAR = 5
+FIRST = {
+    0: (0, 10, 1, 11),
+    1: (0, 10, 1, 11, 100),
+    2: (0, 1, 100),
+    3: (0, 1, 100, 110),
+    4: (0, 10, 1, 11, 100),
+    5: (0, 100),
+    6: (0, 1, 110, 100),
+    7: (100, 110),
+}
+REST = {
+    1: (101, 102, 103),
+    2: (10, 11, 101, 102, 103),
+    3: (101, 111, 102, 112, 103, 113),
+    4: (101, 102, 103),
+    5: (110, 1, 101, 102, 103, 111, 112, 113),
+    6: (111, 101, 112, 113),
+    7: (101, 111, 102, 112, 103, 113),
+}
+LATER = {
+    6: (102, 103),
+}
+TAIL = (2, 1, 3, 2, 2, 1, 0, 0)
 FAR_NEWS = ((0, 2, 4), (7, 5, 3))
 KV_REL = {(2, 2): (3, 3), (3, 2): (2, 1), (4, 2): (5, 3), (4, 1): (5, 2), (6, 3): (4, 1), (6, 2): (7, 3), (7, 2): (6, 1)}
 QD_REL = {(0, 2): (1, 1), (1, 2): (0, 3), (1, 3): (3, 1), (3, 1): (2, 2), (3, 2): (2, 3), (4, 2): (5, 1), (5, 2): (4, 3)}
-ORDER = {
-    0: (0, 110, 112, 111, 113, 120, 130, 131, 132, 121, 133, 122, 123),
-    1: (0, 10, 11, 130, 120, 131, 110, 132, 121, 133, 122, 123, 111, 112, 113),
-    2: (0, 110, 112, 111, 113, 20, 10, 21, 11, 120, 130, 121, 122, 131, 132, 123, 133),
-    3: (0, 10, 11, 130, 20, 131, 30, 21, 132, 31, 110, 120, 133, 111, 112, 121, 122, 113, 123),
-    4: (0, 110, 112, 111, 30, 113, 120, 31, 130, 121, 20, 131, 10, 21, 132, 11, 122, 133, 123),
-    5: (0, 10, 11, 120, 110, 121, 111, 30, 122, 20, 31, 123, 21, 112, 113),
-    6: (110, 112, 111, 30, 113, 20, 31, 0, 10, 21, 11),
-    7: (0, 10, 11, 20, 30, 21, 31),
-}
-
-
-def step_codes(items):
-    codes = []
-    for item in items:
-        if item == 0:
-            codes.append(SEND)
-            continue
-        hop, chunk = item % 100 // 10 - 1, item % 10
-        codes.append(hop * NK + chunk if item < 100 else 3 * NK + hop * NQ + chunk)
-    return codes
+ORDER = ("sghijkopqlrmn", "sabokpgqlrmnhij", "sghijcadboklpmqnr", "sabocpedkqgfrhlimjn", "sghiejkfolpcaqdbmrn", "sabkglhmecfndij", "ghiejcfsadb", "sabcefd")
+
+
+def step_codes(letters):
+    return [ord(x) - ord("a") for x in letters]
 
 
 def targets_of(table, pick):
@@ -76,11 +83,11 @@
 
 
 def body(
-    cu_ref, q_hbm, k_hbm, v_hbm, o_hbm, lse_hbm, do_hbm,
+    cu_hbm, q_hbm, k_hbm, v_hbm, o_hbm, lse_hbm, do_hbm,
     dq_out, dk_out, dv_out,
     q_loc, k_loc, v_loc, o_loc, lse_loc, do_loc, stat_loc, starts,
     k_buf, v_buf, q_buf, do_buf, stat_buf,
-    dqt, dk_acc, dv_acc, in_sem, far_sem,
+    dqt, dk_acc, dv_acc, cu_ref, in_sem, far_sem,
     k_recv, v_recv, q_recv, do_recv, stat_recv,
     kv_own, qd_own, stat_own, kv_rel, qd_rel, stat_rel,
 ):
@@ -102,15 +109,6 @@
     def place(target):
         return {"cpo": target // 4, "cp": target % 4}
 
-    loads = [
-        pltpu.make_async_copy(src, dst, in_sem.at[i])
-        for i, (src, dst) in enumerate(
-            [(k_hbm, k_loc), (v_hbm, v_loc), (q_hbm, q_loc), (do_hbm, do_loc), (o_hbm, o_loc), (lse_hbm, lse_loc)]
-        )
-    ]
-    for load in loads:
-        load.start()
-
     barrier = pltpu.get_barrier_semaphore()
     near = partners()
     for d in range(8):
@@ -118,13 +116,14 @@
         def _(d=d):
             for other in sorted(near[d]):
                 pl.semaphore_signal(barrier, inc=1, device_id=place(other), device_id_type=MESH)
-    lane = lax.broadcasted_iota(jnp.int32, (1, qrows), 1) // 2
-    for h in range(HOPS + 1):
-        pos = lane + (me + h) * rows
-        start = jnp.zeros_like(pos)
-        for j in range(cu_ref.shape[0]):
-            start = jnp.maximum(start, jnp.where(pos >= cu_ref[j], cu_ref[j], 0))
-        starts[h] = start
+    loads = [
+        pltpu.make_async_copy(src, dst, in_sem.at[i])
+        for i, (src, dst) in enumerate(
+            [(k_hbm, k_loc), (v_hbm, v_loc), (q_hbm, q_loc), (do_hbm, do_loc), (o_hbm, o_loc), (lse_hbm, lse_loc), (cu_hbm, cu_ref)]
+        )
+    ]
+    for load in loads:
+        load.start()
     for d in range(8):
         @pl.when(me == d)
         def _(d=d):
@@ -159,33 +158,40 @@
     kv_to = [lut(nth(KV_OWN, n)) for n in range(2)]
     qd_to = [lut(nth(QD_OWN, n)) for n in range(2)]
 
-    def send_kv(n, chunk):
-        for copy in kv_copies(k_loc, v_loc, kv_own.at[n], kv_to[n], chunk):
+    def send(d, item):
+        kind, n, chunk = item // 100, item // 10 % 10, item % 10
+        target, there = (KV_OWN, QD_OWN)[kind][d][n]
+        code = target * 4 + there
+        if kind == 0:
+            copies = kv_copies(k_loc, v_loc, kv_own.at[n], code, chunk)
+        else:
+            copies = qd_copies(q_loc, do_loc, qd_own.at[n], code, chunk)
+        for copy in copies:
             copy.start()
 
-    def send_qd(n, chunk):
-        for copy in qd_copies(q_loc, do_loc, qd_own.at[n], qd_to[n], chunk):
-            copy.start()
-
-    kv_near = [kv_to[0] != NOBODY, (kv_to[1] != NOBODY) & (me != KV_FAR)]
-    qd_near = [qd_to[0] != NOBODY, (qd_to[1] != NOBODY) & (me != QD_FAR)]
+    def send_stat(d, n):
+        target, there = QD_OWN[d][n]
+        stat_copy(stat_loc, stat_own.at[n], target * 4 + there).start()
+
     loads[0].wait()
     loads[1].wait()
-    for chunk in range(NK):
-        for n in range(2):
-            @pl.when(kv_near[n])
-            def _(n=n, chunk=chunk):
-                send_kv(n, chunk)
+    for d in range(8):
+        @pl.when(me == d)
+        def _(d=d):
+            for item in FIRST[d]:
+                if item < 100:
+                    send(d, item)
     loads[2].wait()
     loads[3].wait()
-    for n in range(2):
-        @pl.when(qd_near[n])
-        def _(n=n):
-            send_qd(n, 0)
-    for messenger, far, _ in FAR_NEWS:
-        @pl.when(me == messenger)
-        def _(far=far):
-            pl.semaphore_signal(far_sem, inc=1, device_id=place(far), device_id_type=MESH)
+    for d in range(8):
+        @pl.when(me == d)
+        def _(d=d):
+            for item in FIRST[d]:
+                if item >= 100:
+                    send(d, item)
+            for messenger, far, _ in FAR_NEWS:
+                if messenger == d:
+                    pl.semaphore_signal(far_sem, inc=1, device_id=place(far), device_id_type=MESH)
     loads[4].wait()
     loads[5].wait()
 
@@ -205,31 +211,34 @@
         total = lax.dot_general(ones, hi, dims, preferred_element_type=jnp.float32)
         total = total + lax.dot_general(ones, lo, dims, preferred_element_type=jnp.float32)
         stat_loc[1:2, 256 * j:256 * (j + 1)] = total[0:1]
-    for n in range(2):
-        @pl.when(qd_near[n])
-        def _(n=n):
-            stat_copy(stat_loc, stat_own.at[n], qd_to[n]).start()
-            send_qd(n, 1)
-
-    @pl.when(me == KV_FAR)
-    def _():
-        pl.semaphore_wait(far_sem, 1)
-        for chunk in range(NK):
-            send_kv(1, chunk)
-
-    @pl.when(me == QD_FAR)
-    def _():
-        pl.semaphore_wait(far_sem, 1)
-        send_qd(1, 0)
-        stat_copy(stat_loc, stat_own.at[1], qd_to[1]).start()
-        send_qd(1, 1)
+    for d in range(8):
+        @pl.when(me == d)
+        def _(d=d):
+            for n in range(len(QD_OWN[d])):
+                if not (d == QD_FAR and n == 1):
+                    send_stat(d, n)
+            if d in (KV_FAR, QD_FAR):
+                pl.semaphore_wait(far_sem, 1)
+            if d == QD_FAR:
+                send_stat(d, 1)
+            for item in REST.get(d, ()):
+                send(d, item)
+
+    loads[6].wait()
+    lane = lax.broadcasted_iota(jnp.int32, (1, qrows), 1) // 2
+    for h in range(HOPS + 1):
+        pos = lane + (me + h) * rows
+        start = jnp.zeros_like(pos)
+        for j in range(cu_ref.shape[0]):
+            start = jnp.maximum(start, jnp.where(pos >= cu_ref[j], cu_ref[j], 0))
+        starts[h] = start
 
     def send_later():
-        for chunk in range(2, NQ):
-            for n in range(2):
-                @pl.when(qd_to[n] != NOBODY)
-                def _(n=n, chunk=chunk):
-                    send_qd(n, chunk)
+        for d in LATER:
+            @pl.when(me == d)
+            def _(d=d):
+                for item in LATER[d]:
+                    send(d, item)
 
     def block(k_blk, v_blk, q_blk, do_blk, lse_row, d_row, keep):
         dims = (((1,), (1,)), ((), ()))
@@ -267,21 +276,60 @@
     own_half(half, rows)
     own_half(0, rows // 2)
 
+    def finish_dq():
+        dq_out[...] = (jnp.transpose(dqt[...]) * scale).astype(jnp.bfloat16)
+
+    def kv_block(slot, first_row, count, first_key):
+        cols = pl.ds(first_row, count)
+        keys = pl.ds(first_key, rows - first_key)
+        base = (me - 1 - slot) * rows + first_key
+        keep = key_iota(rows - first_key, count) >= starts[0, :, cols] - base
+        k_blk = k_buf[slot, keys]
+        _, ds_mat = block(k_blk, v_buf[slot, keys], q_loc[cols], do_loc[cols], stat_loc[0:1, cols], stat_loc[1:2, cols], keep)
+        dqt[:, cols] = dqt[:, cols] + dq_term(k_blk, ds_mat)
+
     def kv_unit(slot):
-        base = (me - 1 - slot) * rows
-        keep = key_iota(rows, qrows) >= starts[0] - base
-        k_blk = k_buf[slot]
-        _, ds_mat = block(k_blk, v_buf[slot], q_loc[...], do_loc[...], stat_loc[0:1], stat_loc[1:2], keep)
-        dqt[...] = dqt[...] + dq_term(k_blk, ds_mat)
-
-    def qd_unit(slot, part):
-        cols = pl.ds(pl.multiple_of(part * half, 128), half)
+        @pl.when(slot < HOPS - 1)
+        def _():
+            kv_block(slot, 0, qrows, 0)
+
+        @pl.when(slot == HOPS - 1)
+        def _():
+            kv_block(slot, 0, half, 0)
+            kv_block(slot, half, half, rows // 2)
+
+    def qd_block(slot, first_row, count, first_key):
+        cols = pl.ds(pl.multiple_of(first_row, 128), count)
+        keys = pl.ds(first_key, rows - first_key)
         q_blk = q_buf[slot, cols]
         do_blk = do_buf[slot, cols]
-        keep = key_iota(rows, half) >= starts[slot + 1, :, cols] - me * rows
-        p_low, ds_mat = block(k_loc[...], v_loc[...], q_blk, do_blk, stat_buf[slot, 0:1, cols], stat_buf[slot, 1:2, cols], keep)
-        dv_acc[...] = dv_acc[...] + jnp.dot(p_low, do_blk, preferred_element_type=jnp.float32)
-        dk_acc[...] = dk_acc[...] + jnp.dot(ds_mat, q_blk, preferred_element_type=jnp.float32)
+        keep = key_iota(rows - first_key, count) >= starts[slot + 1, :, cols] - (me * rows + first_key)
+        p_low, ds_mat = block(k_loc[keys], v_loc[keys], q_blk, do_blk, stat_buf[slot, 0:1, cols], stat_buf[slot, 1:2, cols], keep)
+        dv_acc[keys] = dv_acc[keys] + jnp.dot(p_low, do_blk, preferred_element_type=jnp.float32)
+        dk_acc[keys] = dk_acc[keys] + jnp.dot(ds_mat, q_blk, preferred_element_type=jnp.float32)
+
+    def qd_unit(slot, chunk):
+        quarters = (slot == tail) & (chunk >= 2)
+        short = (slot == HOPS - 1) & (chunk == 3)
+
+        @pl.when(quarters)
+        def _():
+            qd_block(slot, chunk * qc_rows, qc_rows, 0)
+
+        @pl.when((chunk % 2 == 1) & jnp.logical_not(quarters) & jnp.logical_not(short))
+        def _():
+            qd_block(slot, (chunk - 1) * qc_rows, half, 0)
+
+        @pl.when(short & jnp.logical_not(quarters))
+        def _():
+            qd_block(slot, half, half, rows // 2)
+
+    tail = lut([t - 1 for t in TAIL])
+    last_kv = lut([max([-1] + [i for i, c in enumerate(step_codes(ORDER[d])) if c < 3 * NK and d > c // NK]) for d in range(8)])
+
+    @pl.when(me == 0)
+    def _():
+        finish_dq()
 
     kv_on = [lut(targets_of(KV_REL, lambda d, h=h: (d, h + 1))) for h in range(HOPS)]
     qd_on = [lut(targets_of(QD_REL, lambda d, h=h: (d, h + 1))) for h in range(HOPS)]
@@ -320,6 +368,10 @@
             def _():
                 kv_unit(slot)
 
+            @pl.when(i == last_kv)
+            def _():
+                finish_dq()
+
         @pl.when((code >= 3 * NK) & (code < SEND))
         def _():
             slot, chunk = (code - 3 * NK) // NQ, (code - 3 * NK) % NQ
@@ -340,9 +392,9 @@
                 def _():
                     stat_copy(stat_buf.at[slot], stat_rel.at[slot], to).start()
 
-            @pl.when((me + slot < 7) & (chunk % 2 == 1))
-            def _():
-                qd_unit(slot, chunk // 2)
+            @pl.when(me + slot < 7)
+            def _():
+                qd_unit(slot, chunk)
 
         @pl.when(code == SEND)
         def _():
@@ -354,7 +406,6 @@
 
     lax.fori_loop(0, steps, step, tuple(packed))
 
-    dq_out[...] = (jnp.transpose(dqt[...]) * scale).astype(jnp.bfloat16)
     dk_out[...] = (dk_acc[...] * scale).astype(jnp.bfloat16)
     dv_out[...] = dv_acc[...].astype(jnp.bfloat16)
 
@@ -396,7 +447,7 @@
             body,
             name="packed_backward",
             out_shape=tuple(pltpu.VMEM(shape, bf) for shape in shapes),
-            in_specs=[pl.BlockSpec(memory_space=pltpu.SMEM)] + [any_spec] * 6,
+            in_specs=[any_spec] * 7,
             out_specs=(vmem_spec,) * 3,
             scratch_shapes=[
                 pltpu.VMEM((qrows, head), bf), pltpu.VMEM((rows, head), bf), pltpu.VMEM((rows, head), bf),
@@ -405,7 +456,7 @@
                 pltpu.VMEM((HOPS, rows, head), bf), pltpu.VMEM((HOPS, rows, head), bf),
                 pltpu.VMEM((HOPS, qrows, head), bf), pltpu.VMEM((HOPS, qrows, head), bf), pltpu.VMEM((HOPS, 2, qrows), f32),
                 pltpu.VMEM((head, qrows), f32), pltpu.VMEM((rows, head), f32), pltpu.VMEM((rows, head), f32),
-                dma((6,)), pltpu.SemaphoreType.REGULAR,
+                pltpu.SMEM(cu_seqlens.shape, jnp.int32), dma((7,)), pltpu.SemaphoreType.REGULAR,
                 dma((HOPS, NK)), dma((HOPS, NK)), dma((HOPS, NQ)), dma((HOPS, NQ)), dma((HOPS,)),
                 dma((2,)), dma((2,)), dma((2,)), dma((HOPS,)), dma((HOPS,)), dma((HOPS,)),
             ],

time: 26.3 us -> 23.4 us (0.89)
  the two profiles are of different devices: /device:TPU:2 before, /device:TPU:1 now
where the time goes in v3:
time: 23.4 us; the launch traced here: 23.3 us
  Pallas kernels  22.7 us (97%)
  between operations  0.64 us (3%)
    pallas_call x1, Pallas kernels, local(): pl.pallas_call(body, name='packed_backward', out_shape=tuple((pltpu.VMEM(...  21.8 us
    pallas_call x1, Pallas kernels, local(): pl.pallas_call(store_body, name='store', out_shape=tuple((jax.ShapeDtypeS...  0.81 us

profile of v3, /device:TPU:1, one launch (start us, length us, event | category | flops | bytes accessed | tf_op | source)
XLA Modules:
  0.0 23.3 jit_solution(16953863645717638594)
XLA Ops:
  0.6 21.8 %packed_backward.1 = (bf16[1024,128]{1,0:T(8,128)(2,1)S(1)}, bf16[512,128]{1,0:T(8,128)(2,1)S(1)}, bf16[512,128]{1,0:T(8,128)(2,1)S(1)}) custom-call(s32[14]{0:T(128)} %cu_hbm.1, bf16[1024,128]{1,0:T(8,128)(2,1)} %bitcast.5, bf16[512,128]{1,0:T(8,128)(2,1)} %k_hbm.1, bf16[512,128]{1,0:T(8,128)(2,1)} %v_hbm.1, bf16[1024,128]{1,0:T(8,128)(2,1)} %bitcast.6, ...), custom_call_target="tpu_custom_call" | custom-call | tf_op jit(solution)/shard_map/packed_backward/pallas_call | solution.py:446
  22.5 0.8 %store.1 = (bf16[1024,128]{1,0:T(8,128)(2,1)}, bf16[512,128]{1,0:T(8,128)(2,1)}, bf16[512,128]{1,0:T(8,128)(2,1)}) custom-call(bf16[1024,128]{1,0:T(8,128)(2,1)S(1)} %get-tuple-element.9.dq_ref, bf16[512,128]{1,0:T(8,128)(2,1)S(1)} %get-tuple-element.10.dk_ref, bf16[512,128]{1,0:T(8,128)(2,1)S(1)} %get-tuple-element.11.dv_ref), custom_call_target="tpu_custom_call" | custom-call | tf_op jit(solution)/shard_map/store/pallas_call | solution.py:465

commit v4 on v3

--- a/solution.py
+++ b/solution.py
@@ -32,7 +32,6 @@
 }
 REST = {
     1: (101, 102, 103),
-    2: (10, 11, 101, 102, 103),
     3: (101, 111, 102, 112, 103, 113),
     4: (101, 102, 103),
     5: (110, 1, 101, 102, 103, 111, 112, 113),
@@ -40,13 +39,14 @@
     7: (101, 111, 102, 112, 103, 113),
 }
 LATER = {
+    2: (10, 11, 101, 102, 103),
     6: (102, 103),
 }
 TAIL = (2, 1, 3, 2, 2, 1, 0, 0)
 FAR_NEWS = ((0, 2, 4), (7, 5, 3))
 KV_REL = {(2, 2): (3, 3), (3, 2): (2, 1), (4, 2): (5, 3), (4, 1): (5, 2), (6, 3): (4, 1), (6, 2): (7, 3), (7, 2): (6, 1)}
 QD_REL = {(0, 2): (1, 1), (1, 2): (0, 3), (1, 3): (3, 1), (3, 1): (2, 2), (3, 2): (2, 3), (4, 2): (5, 1), (5, 2): (4, 3)}
-ORDER = ("sghijkopqlrmn", "sabokpgqlrmnhij", "sghijcadboklpmqnr", "sabocpedkqgfrhlimjn", "sghiejkfolpcaqdbmrn", "sabkglhmecfndij", "ghiejcfsadb", "sabcefd")
+ORDER = ("sghijkopqlrmn", "saobkpqglrmnhij", "sghijcadboklmpqnr", "saobcpedkgqfrhilmjn", "sgheijkfolpcaqdbmrn", "sabkglhmecfndij", "gehijcfsadb", "sabcefd")
 
 
 def step_codes(letters):
@@ -128,6 +128,9 @@
         @pl.when(me == d)
         def _(d=d):
             pl.semaphore_wait(barrier, len(near[d]))
+            for messenger, far, _ in FAR_NEWS:
+                if messenger == d:
+                    pl.semaphore_signal(far_sem, inc=1, device_id=place(far), device_id_type=MESH)
 
     def kv_copies(src_k, src_v, sem, code, chunk):
         target, there = code // 4, code % 4 - 1
@@ -189,9 +192,6 @@
             for item in FIRST[d]:
                 if item >= 100:
                     send(d, item)
-            for messenger, far, _ in FAR_NEWS:
-                if messenger == d:
-                    pl.semaphore_signal(far_sem, inc=1, device_id=place(far), device_id_type=MESH)
     loads[4].wait()
     loads[5].wait()
 
@@ -217,9 +217,8 @@
             for n in range(len(QD_OWN[d])):
                 if not (d == QD_FAR and n == 1):
                     send_stat(d, n)
-            if d in (KV_FAR, QD_FAR):
+            if d == QD_FAR:
                 pl.semaphore_wait(far_sem, 1)
-            if d == QD_FAR:
                 send_stat(d, 1)
             for item in REST.get(d, ()):
                 send(d, item)
@@ -237,6 +236,8 @@
         for d in LATER:
             @pl.when(me == d)
             def _(d=d):
+                if d == KV_FAR:
+                    pl.semaphore_wait(far_sem, 1)
                 for item in LATER[d]:
                     send(d, item)
 

time: 23.4 us -> 23.4 us (level)
  no operation moved by 1% of the time
where the time goes in v4:
time: 23.4 us; the launch traced here: 23.3 us
  Pallas kernels  22.7 us (97%)
  between operations  0.64 us (3%)
    pallas_call x1, Pallas kernels, local(): pl.pallas_call(body, name='packed_backward', out_shape=tuple((pltpu.VMEM(...  21.8 us
    pallas_call x1, Pallas kernels, local(): pl.pallas_call(store_body, name='store', out_shape=tuple((jax.ShapeDtypeS...  0.81 us

profile of v4, /device:TPU:1, one launch (start us, length us, event | category | flops | bytes accessed | tf_op | source)
XLA Modules:
  0.0 23.3 jit_solution(363536988024898165)
XLA Ops:
  0.6 21.8 %packed_backward.1 = (bf16[1024,128]{1,0:T(8,128)(2,1)S(1)}, bf16[512,128]{1,0:T(8,128)(2,1)S(1)}, bf16[512,128]{1,0:T(8,128)(2,1)S(1)}) custom-call(s32[14]{0:T(128)} %cu_hbm.1, bf16[1024,128]{1,0:T(8,128)(2,1)} %bitcast.5, bf16[512,128]{1,0:T(8,128)(2,1)} %k_hbm.1, bf16[512,128]{1,0:T(8,128)(2,1)} %v_hbm.1, bf16[1024,128]{1,0:T(8,128)(2,1)} %bitcast.6, ...), custom_call_target="tpu_custom_call" | custom-call | tf_op jit(solution)/shard_map/packed_backward/pallas_call | solution.py:447
  22.5 0.8 %store.1 = (bf16[1024,128]{1,0:T(8,128)(2,1)}, bf16[512,128]{1,0:T(8,128)(2,1)}, bf16[512,128]{1,0:T(8,128)(2,1)}) custom-call(bf16[1024,128]{1,0:T(8,128)(2,1)S(1)} %get-tuple-element.9.dq_ref, bf16[512,128]{1,0:T(8,128)(2,1)S(1)} %get-tuple-element.10.dk_ref, bf16[512,128]{1,0:T(8,128)(2,1)S(1)} %get-tuple-element.11.dv_ref), custom_call_target="tpu_custom_call" | custom-call | tf_op jit(solution)/shard_map/store/pallas_call | solution.py:466

commit v5 on v4

--- a/solution.py
+++ b/solution.py
@@ -32,21 +32,23 @@
 }
 REST = {
     1: (101, 102, 103),
-    3: (101, 111, 102, 112, 103, 113),
+    3: (101, 111, 102, 103),
     4: (101, 102, 103),
     5: (110, 1, 101, 102, 103, 111, 112, 113),
-    6: (111, 101, 112, 113),
-    7: (101, 111, 102, 112, 103, 113),
+    6: (111, 112, 113, 101),
+    7: (101, 111, 102, 103),
 }
 LATER = {
     2: (10, 11, 101, 102, 103),
+    3: (112, 113),
     6: (102, 103),
+    7: (112, 113),
 }
-TAIL = (2, 1, 3, 2, 2, 1, 0, 0)
+TAIL = (2, 3, 0, 0, 2, 3, 0, 0)
 FAR_NEWS = ((0, 2, 4), (7, 5, 3))
 KV_REL = {(2, 2): (3, 3), (3, 2): (2, 1), (4, 2): (5, 3), (4, 1): (5, 2), (6, 3): (4, 1), (6, 2): (7, 3), (7, 2): (6, 1)}
 QD_REL = {(0, 2): (1, 1), (1, 2): (0, 3), (1, 3): (3, 1), (3, 1): (2, 2), (3, 2): (2, 3), (4, 2): (5, 1), (5, 2): (4, 3)}
-ORDER = ("sghijkopqlrmn", "saobkpqglrmnhij", "sghijcadboklmpqnr", "saobcpedkgqfrhilmjn", "sgheijkfolpcaqdbmrn", "sabkglhmecfndij", "gehijcfsadb", "sabcefd")
+ORDER = ("sghijkoplmnqr", "saobkpqlrghminj", "sghijcadbkolpmqnr", "abcedfsgkhlimjnopqr", "sgheijkfolpcadbmnqr", "sabkglhecfdminj", "gehijcfsadb", "abcefds")
 
 
 def step_codes(letters):
@@ -310,7 +312,7 @@
         dk_acc[keys] = dk_acc[keys] + jnp.dot(ds_mat, q_blk, preferred_element_type=jnp.float32)
 
     def qd_unit(slot, chunk):
-        quarters = (slot == tail) & (chunk >= 2)
+        quarters = (pick(tail, slot) == 1) & (chunk >= 2)
         short = (slot == HOPS - 1) & (chunk == 3)
 
         @pl.when(quarters)
@@ -325,7 +327,7 @@
         def _():
             qd_block(slot, half, half, rows // 2)
 
-    tail = lut([t - 1 for t in TAIL])
+    tail = [lut([(t >> h) % 2 for t in TAIL]) for h in range(HOPS)]
     last_kv = lut([max([-1] + [i for i, c in enumerate(step_codes(ORDER[d])) if c < 3 * NK and d > c // NK]) for d in range(8)])
 
     @pl.when(me == 0)

time: 23.4 us -> 23.7 us (1.013)
  the two profiles are of different devices: /device:TPU:1 before, /device:TPU:0 now
where the time goes in v5:
time: 23.7 us; the launch traced here: 23.6 us
  Pallas kernels  22.9 us (97%)
  between operations  0.64 us (3%)
    pallas_call x1, Pallas kernels, local(): pl.pallas_call(body, name='packed_backward', out_shape=tuple((pltpu.VMEM(...  22.1 us
    pallas_call x1, Pallas kernels, local(): pl.pallas_call(store_body, name='store', out_shape=tuple((jax.ShapeDtypeS...  0.81 us

profile of v5, /device:TPU:0, one launch (start us, length us, event | category | flops | bytes accessed | tf_op | source)
XLA Modules:
  0.0 23.6 jit_solution(6159772024015586980)
XLA Ops:
  0.6 22.1 %packed_backward.1 = (bf16[1024,128]{1,0:T(8,128)(2,1)S(1)}, bf16[512,128]{1,0:T(8,128)(2,1)S(1)}, bf16[512,128]{1,0:T(8,128)(2,1)S(1)}) custom-call(s32[14]{0:T(128)} %cu_hbm.1, bf16[1024,128]{1,0:T(8,128)(2,1)} %bitcast.5, bf16[512,128]{1,0:T(8,128)(2,1)} %k_hbm.1, bf16[512,128]{1,0:T(8,128)(2,1)} %v_hbm.1, bf16[1024,128]{1,0:T(8,128)(2,1)} %bitcast.6, ...), custom_call_target="tpu_custom_call" | custom-call | tf_op jit(solution)/shard_map/packed_backward/pallas_call | solution.py:449
  22.7 0.8 %store.1 = (bf16[1024,128]{1,0:T(8,128)(2,1)}, bf16[512,128]{1,0:T(8,128)(2,1)}, bf16[512,128]{1,0:T(8,128)(2,1)}) custom-call(bf16[1024,128]{1,0:T(8,128)(2,1)S(1)} %get-tuple-element.9.dq_ref, bf16[512,128]{1,0:T(8,128)(2,1)S(1)} %get-tuple-element.10.dk_ref, bf16[512,128]{1,0:T(8,128)(2,1)S(1)} %get-tuple-element.11.dv_ref), custom_call_target="tpu_custom_call" | custom-call | tf_op jit(solution)/shard_map/store/pallas_call | solution.py:468

commit v6 on v5

--- a/solution.py
+++ b/solution.py
@@ -18,13 +18,11 @@
 
 KV_OWN = {0: [(1, 1), (2, 2)], 1: [(3, 2), (4, 3)], 2: [(3, 1), (4, 2)], 3: [(6, 3)], 4: [(5, 1), (6, 2)], 5: [(7, 2)], 6: [(7, 1)], 7: []}
 QD_OWN = {0: [], 1: [(0, 1)], 2: [(0, 2)], 3: [(2, 1), (1, 2)], 4: [(1, 3)], 5: [(4, 1), (3, 2)], 6: [(4, 2), (3, 3)], 7: [(6, 1), (5, 2)]}
-KV_FAR = 2
-QD_FAR = 5
 FIRST = {
     0: (0, 10, 1, 11),
-    1: (0, 10, 1, 11, 100),
+    1: (0, 1, 100),
     2: (0, 1, 100),
-    3: (0, 1, 100, 110),
+    3: (100, 110),
     4: (0, 10, 1, 11, 100),
     5: (0, 100),
     6: (0, 1, 110, 100),
@@ -32,23 +30,28 @@
 }
 REST = {
     1: (101, 102, 103),
-    3: (101, 111, 102, 103),
+    2: (),
+    3: (101, 111, 102, 112, 103),
     4: (101, 102, 103),
-    5: (110, 1, 101, 102, 103, 111, 112, 113),
+    5: (110, 101, 1, 111, 112, 113, 102, 103),
     6: (111, 112, 113, 101),
-    7: (101, 111, 102, 103),
+    7: (101, 111, 102, 112, 103),
+}
+AFTER = {
+    1: (10, 11),
+    2: (10, 11, 101, 102, 103),
+    3: (0, 1),
 }
 LATER = {
-    2: (10, 11, 101, 102, 103),
-    3: (112, 113),
+    3: (113,),
     6: (102, 103),
-    7: (112, 113),
+    7: (113,),
 }
 TAIL = (2, 3, 0, 0, 2, 3, 0, 0)
-FAR_NEWS = ((0, 2, 4), (7, 5, 3))
+GO = ((4, 1), (4, 2), (6, 3))
 KV_REL = {(2, 2): (3, 3), (3, 2): (2, 1), (4, 2): (5, 3), (4, 1): (5, 2), (6, 3): (4, 1), (6, 2): (7, 3), (7, 2): (6, 1)}
 QD_REL = {(0, 2): (1, 1), (1, 2): (0, 3), (1, 3): (3, 1), (3, 1): (2, 2), (3, 2): (2, 3), (4, 2): (5, 1), (5, 2): (4, 3)}
-ORDER = ("sghijkoplmnqr", "saobkpqlrghminj", "sghijcadbkolpmqnr", "abcedfsgkhlimjnopqr", "sgheijkfolpcadbmnqr", "sabkglhecfdminj", "gehijcfsadb", "abcefds")
+ORDER = ("ghijkoplmqnr", "aobkpqlrghminj", "ghijcadbkolpmqnr", "abcedfsgkhlimjnopqr", "gheijkfolpcadbmqnr", "abkglhecfdminj", "ghijceafsdb", "abcefds")
 
 
 def step_codes(letters):
@@ -66,21 +69,12 @@
 
 def partners():
     near = {d: set() for d in range(8)}
-    for table in (KV_OWN, QD_OWN):
-        for d, pairs in table.items():
-            for n, (target, _) in enumerate(pairs):
-                if n == 1 and d == (KV_FAR if table is KV_OWN else QD_FAR):
-                    continue
-                near[d].add(target)
-                near[target].add(d)
-    for messenger, far, target in FAR_NEWS:
-        for other in (far, target):
-            near[messenger].add(other)
-            near[other].add(messenger)
-    for table in (KV_REL, QD_REL):
-        for (d, _), (target, _) in table.items():
-            near[d].add(target)
-            near[target].add(d)
+    pairs = [(d, target) for table in (KV_OWN, QD_OWN) for d in table for target, _ in table[d]]
+    pairs += [(d, target) for table in (KV_REL, QD_REL) for (d, _), (target, _) in table.items()]
+    for a, b in pairs:
+        for here, there in ((a, b), (b, a)):
+            if here >= 4 or there < 4:
+                near[here].add(there)
     return near
 
 
@@ -89,7 +83,7 @@
     dq_out, dk_out, dv_out,
     q_loc, k_loc, v_loc, o_loc, lse_loc, do_loc, stat_loc, starts,
     k_buf, v_buf, q_buf, do_buf, stat_buf,
-    dqt, dk_acc, dv_acc, cu_ref, in_sem, far_sem,
+    dqt, dk_acc, dv_acc, cu_ref, in_sem, go_sem,
     k_recv, v_recv, q_recv, do_recv, stat_recv,
     kv_own, qd_own, stat_own, kv_rel, qd_rel, stat_rel,
 ):
@@ -116,7 +110,7 @@
     for d in range(8):
         @pl.when(me == d)
         def _(d=d):
-            for other in sorted(near[d]):
+            for other in [x for x in range(8) if d in near[x]]:
                 pl.semaphore_signal(barrier, inc=1, device_id=place(other), device_id_type=MESH)
     loads = [
         pltpu.make_async_copy(src, dst, in_sem.at[i])
@@ -130,9 +124,9 @@
         @pl.when(me == d)
         def _(d=d):
             pl.semaphore_wait(barrier, len(near[d]))
-            for messenger, far, _ in FAR_NEWS:
-                if messenger == d:
-                    pl.semaphore_signal(far_sem, inc=1, device_id=place(far), device_id_type=MESH)
+            for teller, told in GO:
+                if teller == d:
+                    pl.semaphore_signal(go_sem, inc=1, device_id=place(told), device_id_type=MESH)
 
     def kv_copies(src_k, src_v, sem, code, chunk):
         target, there = code // 4, code % 4 - 1
@@ -217,11 +211,7 @@
         @pl.when(me == d)
         def _(d=d):
             for n in range(len(QD_OWN[d])):
-                if not (d == QD_FAR and n == 1):
-                    send_stat(d, n)
-            if d == QD_FAR:
-                pl.semaphore_wait(far_sem, 1)
-                send_stat(d, 1)
+                send_stat(d, n)
             for item in REST.get(d, ()):
                 send(d, item)
 
@@ -238,8 +228,6 @@
         for d in LATER:
             @pl.when(me == d)
             def _(d=d):
-                if d == KV_FAR:
-                    pl.semaphore_wait(far_sem, 1)
                 for item in LATER[d]:
                     send(d, item)
 
@@ -277,6 +265,12 @@
             dk_acc[0:keys] = dk_acc[0:keys] + dk_new
 
     own_half(half, rows)
+    for d in AFTER:
+        @pl.when(me == d)
+        def _(d=d):
+            pl.semaphore_wait(go_sem, 1)
+            for item in AFTER[d]:
+                send(d, item)
     own_half(0, rows // 2)
 
     def finish_dq():

time: 23.7 us -> 23.5 us (level)
  no operation moved by 1% of the time
where the time goes in v6:
time: 23.5 us; the launch traced here: 23.4 us
  Pallas kernels  22.7 us (97%)
  between operations  0.64 us (3%)
    pallas_call x1, Pallas kernels, local(): pl.pallas_call(body, name='packed_backward', out_shape=tuple((pltpu.VMEM(...  21.9 us
    pallas_call x1, Pallas kernels, local(): pl.pallas_call(store_body, name='store', out_shape=tuple((jax.ShapeDtypeS...  0.81 us

profile of v6, /device:TPU:0, one launch (start us, length us, event | category | flops | bytes accessed | tf_op | source)
XLA Modules:
  0.0 23.4 jit_solution(6785126466715150168)
XLA Ops:
  0.6 21.9 %packed_backward.1 = (bf16[1024,128]{1,0:T(8,128)(2,1)S(1)}, bf16[512,128]{1,0:T(8,128)(2,1)S(1)}, bf16[512,128]{1,0:T(8,128)(2,1)S(1)}) custom-call(s32[14]{0:T(128)} %cu_hbm.1, bf16[1024,128]{1,0:T(8,128)(2,1)} %bitcast.5, bf16[512,128]{1,0:T(8,128)(2,1)} %k_hbm.1, bf16[512,128]{1,0:T(8,128)(2,1)} %v_hbm.1, bf16[1024,128]{1,0:T(8,128)(2,1)} %bitcast.6, ...), custom_call_target="tpu_custom_call" | custom-call | tf_op jit(solution)/shard_map/packed_backward/pallas_call | solution.py:443
  22.6 0.8 %store.1 = (bf16[1024,128]{1,0:T(8,128)(2,1)}, bf16[512,128]{1,0:T(8,128)(2,1)}, bf16[512,128]{1,0:T(8,128)(2,1)}) custom-call(bf16[1024,128]{1,0:T(8,128)(2,1)S(1)} %get-tuple-element.9.dq_ref, bf16[512,128]{1,0:T(8,128)(2,1)S(1)} %get-tuple-element.10.dk_ref, bf16[512,128]{1,0:T(8,128)(2,1)S(1)} %get-tuple-element.11.dv_ref), custom_call_target="tpu_custom_call" | custom-call | tf_op jit(solution)/shard_map/store/pallas_call | solution.py:462

commit v7 on v6

--- a/solution.py
+++ b/solution.py
@@ -39,7 +39,7 @@
 }
 AFTER = {
     1: (10, 11),
-    2: (10, 11, 101, 102, 103),
+    2: (10, 101, 102, 103, 11),
     3: (0, 1),
 }
 LATER = {
@@ -51,7 +51,7 @@
 GO = ((4, 1), (4, 2), (6, 3))
 KV_REL = {(2, 2): (3, 3), (3, 2): (2, 1), (4, 2): (5, 3), (4, 1): (5, 2), (6, 3): (4, 1), (6, 2): (7, 3), (7, 2): (6, 1)}
 QD_REL = {(0, 2): (1, 1), (1, 2): (0, 3), (1, 3): (3, 1), (3, 1): (2, 2), (3, 2): (2, 3), (4, 2): (5, 1), (5, 2): (4, 3)}
-ORDER = ("ghijkoplmqnr", "aobkpqlrghminj", "ghijcadbkolpmqnr", "abcedfsgkhlimjnopqr", "gheijkfolpcadbmqnr", "abkglhecfdminj", "ghijceafsdb", "abcefds")
+ORDER = ("ghijkoplmqnr", "aobkpqlrghminj", "ghijcadbkolpmqnr", "abcedfsgkhlimjnopqr", "gheijkfolpcabmnqdr", "abkglhecdminjf", "ghijceafsdb", "abcefds")
 
 
 def step_codes(letters):

time: 23.5 us -> 22.8 us (0.970)
  the two profiles are of different devices: /device:TPU:0 before, /device:TPU:5 now
where the time goes in v7:
time: 22.8 us; the launch traced here: 22.7 us
  Pallas kernels  22 us (96%)
  between operations  0.64 us (3%)
    pallas_call x1, Pallas kernels, local(): pl.pallas_call(body, name='packed_backward', out_shape=tuple((pltpu.VMEM(...  21.2 us
    pallas_call x1, Pallas kernels, local(): pl.pallas_call(store_body, name='store', out_shape=tuple((jax.ShapeDtypeS...  0.81 us

profile of v7, /device:TPU:5, one launch (start us, length us, event | category | flops | bytes accessed | tf_op | source)
XLA Modules:
  0.0 22.7 jit_solution(16578841635529905438)
XLA Ops:
  0.6 21.2 %packed_backward.1 = (bf16[1024,128]{1,0:T(8,128)(2,1)S(1)}, bf16[512,128]{1,0:T(8,128)(2,1)S(1)}, bf16[512,128]{1,0:T(8,128)(2,1)S(1)}) custom-call(s32[14]{0:T(128)} %cu_hbm.1, bf16[1024,128]{1,0:T(8,128)(2,1)} %bitcast.5, bf16[512,128]{1,0:T(8,128)(2,1)} %k_hbm.1, bf16[512,128]{1,0:T(8,128)(2,1)} %v_hbm.1, bf16[1024,128]{1,0:T(8,128)(2,1)} %bitcast.6, ...), custom_call_target="tpu_custom_call" | custom-call | tf_op jit(solution)/shard_map/packed_backward/pallas_call | solution.py:443
  21.9 0.8 %store.1 = (bf16[1024,128]{1,0:T(8,128)(2,1)}, bf16[512,128]{1,0:T(8,128)(2,1)}, bf16[512,128]{1,0:T(8,128)(2,1)}) custom-call(bf16[1024,128]{1,0:T(8,128)(2,1)S(1)} %get-tuple-element.9.dq_ref, bf16[512,128]{1,0:T(8,128)(2,1)S(1)} %get-tuple-element.10.dk_ref, bf16[512,128]{1,0:T(8,128)(2,1)S(1)} %get-tuple-element.11.dv_ref), custom_call_target="tpu_custom_call" | custom-call | tf_op jit(solution)/shard_map/store/pallas_call | solution.py:462

commit v8 on v7

--- a/solution.py
+++ b/solution.py
@@ -16,7 +16,7 @@
 NOBODY = 63
 SEND = 18
 
-KV_OWN = {0: [(1, 1), (2, 2)], 1: [(3, 2), (4, 3)], 2: [(3, 1), (4, 2)], 3: [(6, 3)], 4: [(5, 1), (6, 2)], 5: [(7, 2)], 6: [(7, 1)], 7: []}
+KV_OWN = {0: [(1, 1), (2, 2)], 1: [(3, 2), (4, 3)], 2: [(3, 1), (5, 3)], 3: [(6, 3)], 4: [(5, 1), (6, 2)], 5: [(7, 2)], 6: [(7, 1)], 7: []}
 QD_OWN = {0: [], 1: [(0, 1)], 2: [(0, 2)], 3: [(2, 1), (1, 2)], 4: [(1, 3)], 5: [(4, 1), (3, 2)], 6: [(4, 2), (3, 3)], 7: [(6, 1), (5, 2)]}
 FIRST = {
     0: (0, 10, 1, 11),
@@ -48,10 +48,11 @@
     7: (113,),
 }
 TAIL = (2, 3, 0, 0, 2, 3, 0, 0)
-GO = ((4, 1), (4, 2), (6, 3))
-KV_REL = {(2, 2): (3, 3), (3, 2): (2, 1), (4, 2): (5, 3), (4, 1): (5, 2), (6, 3): (4, 1), (6, 2): (7, 3), (7, 2): (6, 1)}
+LATE_KEYS = 4
+GO = ((4, 1), (5, 2), (6, 3))
+KV_REL = {(2, 2): (3, 3), (3, 2): (2, 1), (5, 3): (4, 2), (4, 1): (5, 2), (6, 3): (4, 1), (6, 2): (7, 3), (7, 2): (6, 1)}
 QD_REL = {(0, 2): (1, 1), (1, 2): (0, 3), (1, 3): (3, 1), (3, 1): (2, 2), (3, 2): (2, 3), (4, 2): (5, 1), (5, 2): (4, 3)}
-ORDER = ("ghijkoplmqnr", "aobkpqlrghminj", "ghijcadbkolpmqnr", "abcedfsgkhlimjnopqr", "gheijkfolpcabmnqdr", "abkglhecdminjf", "ghijceafsdb", "abcefds")
+ORDER = ("ghijkoplmqnr", "aobkpqlrghminj", "ghijcadbkolpmqnr", "abcedfsgkhlimjnopqr", "gheijkfolpcabmnqrd", "abkglhecdminfj", "ghijceafsdb", "abcefds")
 
 
 def step_codes(letters):
@@ -276,24 +277,34 @@
     def finish_dq():
         dq_out[...] = (jnp.transpose(dqt[...]) * scale).astype(jnp.bfloat16)
 
-    def kv_block(slot, first_row, count, first_key):
-        cols = pl.ds(first_row, count)
-        keys = pl.ds(first_key, rows - first_key)
+    def kv_block(slot, count, first_key, width):
+        cols = pl.ds(0, count)
+        keys = pl.ds(first_key, width)
         base = (me - 1 - slot) * rows + first_key
-        keep = key_iota(rows - first_key, count) >= starts[0, :, cols] - base
+        keep = key_iota(width, count) >= starts[0, :, cols] - base
         k_blk = k_buf[slot, keys]
         _, ds_mat = block(k_blk, v_buf[slot, keys], q_loc[cols], do_loc[cols], stat_loc[0:1, cols], stat_loc[1:2, cols], keep)
         dqt[:, cols] = dqt[:, cols] + dq_term(k_blk, ds_mat)
 
-    def kv_unit(slot):
-        @pl.when(slot < HOPS - 1)
-        def _():
-            kv_block(slot, 0, qrows, 0)
-
-        @pl.when(slot == HOPS - 1)
-        def _():
-            kv_block(slot, 0, half, 0)
-            kv_block(slot, half, half, rows // 2)
+    def kv_unit(slot, chunk):
+        far = slot == HOPS - 1
+        late = (slot == 1) & (me == LATE_KEYS)
+
+        @pl.when(far & (chunk == 0))
+        def _():
+            kv_block(slot, half, 0, kc_rows)
+
+        @pl.when(late & (chunk == 0))
+        def _():
+            kv_block(slot, qrows, 0, kc_rows)
+
+        @pl.when((far | late) & (chunk == 1))
+        def _():
+            kv_block(slot, qrows, kc_rows, kc_rows)
+
+        @pl.when(jnp.logical_not(far | late) & (chunk == 1))
+        def _():
+            kv_block(slot, qrows, 0, rows)
 
     def qd_block(slot, first_row, count, first_key):
         cols = pl.ds(pl.multiple_of(first_row, 128), count)
@@ -361,9 +372,9 @@
                 for copy in kv_copies(k_buf.at[slot], v_buf.at[slot], kv_rel.at[slot], to, chunk):
                     copy.start()
 
-            @pl.when((me > slot) & (chunk == NK - 1))
-            def _():
-                kv_unit(slot)
+            @pl.when(me > slot)
+            def _():
+                kv_unit(slot, chunk)
 
             @pl.when(i == last_kv)
             def _():

time: 22.8 us -> 22.6 us (level)
  no operation moved by 1% of the time
where the time goes in v8:
time: 22.6 us; the launch traced here: 22.5 us
  Pallas kernels  21.8 us (96%)
  between operations  0.64 us (3%)
    pallas_call x1, Pallas kernels, local(): pl.pallas_call(body, name='packed_backward', out_shape=tuple((pltpu.VMEM(...  21 us
    pallas_call x1, Pallas kernels, local(): pl.pallas_call(store_body, name='store', out_shape=tuple((jax.ShapeDtypeS...  0.81 us

profile of v8, /device:TPU:5, one launch (start us, length us, event | category | flops | bytes accessed | tf_op | source)
XLA Modules:
  0.0 22.5 jit_solution(9465087746302597591)
XLA Ops:
  0.6 21.0 %packed_backward.1 = (bf16[1024,128]{1,0:T(8,128)(2,1)S(1)}, bf16[512,128]{1,0:T(8,128)(2,1)S(1)}, bf16[512,128]{1,0:T(8,128)(2,1)S(1)}) custom-call(s32[14]{0:T(128)} %cu_hbm.1, bf16[1024,128]{1,0:T(8,128)(2,1)} %bitcast.5, bf16[512,128]{1,0:T(8,128)(2,1)} %k_hbm.1, bf16[512,128]{1,0:T(8,128)(2,1)} %v_hbm.1, bf16[1024,128]{1,0:T(8,128)(2,1)} %bitcast.6, ...), custom_call_target="tpu_custom_call" | custom-call | tf_op jit(solution)/shard_map/packed_backward/pallas_call | solution.py:454
  21.7 0.8 %store.1 = (bf16[1024,128]{1,0:T(8,128)(2,1)}, bf16[512,128]{1,0:T(8,128)(2,1)}, bf16[512,128]{1,0:T(8,128)(2,1)}) custom-call(bf16[1024,128]{1,0:T(8,128)(2,1)S(1)} %get-tuple-element.9.dq_ref, bf16[512,128]{1,0:T(8,128)(2,1)S(1)} %get-tuple-element.10.dk_ref, bf16[512,128]{1,0:T(8,128)(2,1)S(1)} %get-tuple-element.11.dv_ref), custom_call_target="tpu_custom_call" | custom-call | tf_op jit(solution)/shard_map/store/pallas_call | solution.py:473

commit v9 on v8

--- a/solution.py
+++ b/solution.py
@@ -17,7 +17,7 @@
 SEND = 18
 
 KV_OWN = {0: [(1, 1), (2, 2)], 1: [(3, 2), (4, 3)], 2: [(3, 1), (5, 3)], 3: [(6, 3)], 4: [(5, 1), (6, 2)], 5: [(7, 2)], 6: [(7, 1)], 7: []}
-QD_OWN = {0: [], 1: [(0, 1)], 2: [(0, 2)], 3: [(2, 1), (1, 2)], 4: [(1, 3)], 5: [(4, 1), (3, 2)], 6: [(4, 2), (3, 3)], 7: [(6, 1), (5, 2)]}
+QD_OWN = {0: [], 1: [(0, 1)], 2: [(0, 2)], 3: [(2, 1), (1, 2)], 4: [(1, 3)], 5: [(4, 1), (3, 2)], 6: [(5, 1), (3, 3)], 7: [(6, 1), (5, 2)]}
 FIRST = {
     0: (0, 10, 1, 11),
     1: (0, 1, 100),
@@ -51,8 +51,8 @@
 LATE_KEYS = 4
 GO = ((4, 1), (5, 2), (6, 3))
 KV_REL = {(2, 2): (3, 3), (3, 2): (2, 1), (5, 3): (4, 2), (4, 1): (5, 2), (6, 3): (4, 1), (6, 2): (7, 3), (7, 2): (6, 1)}
-QD_REL = {(0, 2): (1, 1), (1, 2): (0, 3), (1, 3): (3, 1), (3, 1): (2, 2), (3, 2): (2, 3), (4, 2): (5, 1), (5, 2): (4, 3)}
-ORDER = ("ghijkoplmqnr", "aobkpqlrghminj", "ghijcadbkolpmqnr", "abcedfsgkhlimjnopqr", "gheijkfolpcabmnqrd", "abkglhecdminfj", "ghijceafsdb", "abcefds")
+QD_REL = {(0, 2): (1, 1), (1, 2): (0, 3), (1, 3): (3, 1), (3, 1): (2, 2), (3, 2): (2, 3), (5, 1): (4, 2), (5, 2): (4, 3)}
+ORDER = ("ghijkoplmqnr", "aobkpqlrghminj", "ghijcadbkolpmqnr", "abcedfsgkhlimjnopqr", "gheijkfolpcabmqnrd", "abkglhecdminfj", "ghijceafsdb", "abcefds")
 
 
 def step_codes(letters):

time: 22.6 us -> 24.2 us (1.071)
  the two profiles are of different devices: /device:TPU:5 before, /device:TPU:4 now
where the time goes in v9:
time: 24.2 us; the launch traced here: 24.1 us
  Pallas kernels  23.4 us (97%)
  between operations  0.64 us (3%)
    pallas_call x1, Pallas kernels, local(): pl.pallas_call(body, name='packed_backward', out_shape=tuple((pltpu.VMEM(...  22.6 us
    pallas_call x1, Pallas kernels, local(): pl.pallas_call(store_body, name='store', out_shape=tuple((jax.ShapeDtypeS...  0.81 us

profile of v9, /device:TPU:4, one launch (start us, length us, event | category | flops | bytes accessed | tf_op | source)
XLA Modules:
  0.0 24.1 jit_solution(9788688317571371009)
XLA Ops:
  0.6 22.6 %packed_backward.1 = (bf16[1024,128]{1,0:T(8,128)(2,1)S(1)}, bf16[512,128]{1,0:T(8,128)(2,1)S(1)}, bf16[512,128]{1,0:T(8,128)(2,1)S(1)}) custom-call(s32[14]{0:T(128)} %cu_hbm.1, bf16[1024,128]{1,0:T(8,128)(2,1)} %bitcast.5, bf16[512,128]{1,0:T(8,128)(2,1)} %k_hbm.1, bf16[512,128]{1,0:T(8,128)(2,1)} %v_hbm.1, bf16[1024,128]{1,0:T(8,128)(2,1)} %bitcast.6, ...), custom_call_target="tpu_custom_call" | custom-call | tf_op jit(solution)/shard_map/packed_backward/pallas_call | solution.py:454
  23.3 0.8 %store.1 = (bf16[1024,128]{1,0:T(8,128)(2,1)}, bf16[512,128]{1,0:T(8,128)(2,1)}, bf16[512,128]{1,0:T(8,128)(2,1)}) custom-call(bf16[1024,128]{1,0:T(8,128)(2,1)S(1)} %get-tuple-element.9.dq_ref, bf16[512,128]{1,0:T(8,128)(2,1)S(1)} %get-tuple-element.10.dk_ref, bf16[512,128]{1,0:T(8,128)(2,1)S(1)} %get-tuple-element.11.dv_ref), custom_call_target="tpu_custom_call" | custom-call | tf_op jit(solution)/shard_map/store/pallas_call | solution.py:473

commit v10 on v8

--- a/solution.py
+++ b/solution.py
@@ -116,7 +116,11 @@
     loads = [
         pltpu.make_async_copy(src, dst, in_sem.at[i])
         for i, (src, dst) in enumerate(
-            [(k_hbm, k_loc), (v_hbm, v_loc), (q_hbm, q_loc), (do_hbm, do_loc), (o_hbm, o_loc), (lse_hbm, lse_loc), (cu_hbm, cu_ref)]
+            [
+                (q_hbm.at[0:qc_rows], q_loc.at[0:qc_rows]), (do_hbm.at[0:qc_rows], do_loc.at[0:qc_rows]), (k_hbm, k_loc), (v_hbm, v_loc),
+                (q_hbm.at[qc_rows:], q_loc.at[qc_rows:]), (do_hbm.at[qc_rows:], do_loc.at[qc_rows:]), (o_hbm, o_loc), (lse_hbm, lse_loc),
+                (cu_hbm, cu_ref),
+            ]
         )
     ]
     for load in loads:
@@ -179,7 +183,7 @@
         @pl.when(me == d)
         def _(d=d):
             for item in FIRST[d]:
-                if item < 100:
+                if item >= 100:
                     send(d, item)
     loads[2].wait()
     loads[3].wait()
@@ -187,10 +191,10 @@
         @pl.when(me == d)
         def _(d=d):
             for item in FIRST[d]:
-                if item >= 100:
+                if item < 100:
                     send(d, item)
-    loads[4].wait()
-    loads[5].wait()
+    for load in loads[4:8]:
+        load.wait()
 
     wide = lax.broadcasted_iota(jnp.int32, (2, 128), 1)
     for j in range(qrows // 128):
@@ -216,7 +220,7 @@
             for item in REST.get(d, ()):
                 send(d, item)
 
-    loads[6].wait()
+    loads[8].wait()
     lane = lax.broadcasted_iota(jnp.int32, (1, qrows), 1) // 2
     for h in range(HOPS + 1):
         pos = lane + (me + h) * rows
@@ -464,7 +468,7 @@
                 pltpu.VMEM((HOPS, rows, head), bf), pltpu.VMEM((HOPS, rows, head), bf),
                 pltpu.VMEM((HOPS, qrows, head), bf), pltpu.VMEM((HOPS, qrows, head), bf), pltpu.VMEM((HOPS, 2, qrows), f32),
                 pltpu.VMEM((head, qrows), f32), pltpu.VMEM((rows, head), f32), pltpu.VMEM((rows, head), f32),
-                pltpu.SMEM(cu_seqlens.shape, jnp.int32), dma((7,)), pltpu.SemaphoreType.REGULAR,
+                pltpu.SMEM(cu_seqlens.shape, jnp.int32), dma((9,)), pltpu.SemaphoreType.REGULAR,
                 dma((HOPS, NK)), dma((HOPS, NK)), dma((HOPS, NQ)), dma((HOPS, NQ)), dma((HOPS,)),
                 dma((2,)), dma((2,)), dma((2,)), dma((HOPS,)), dma((HOPS,)), dma((HOPS,)),
             ],

time: 22.6 us -> 22.3 us (0.987)
    pallas_call x1, Pallas kernels: 21 us -> 20.8 us  [local(): pl.pallas_call(body, name='packed_backward', out_shape=tuple((pltpu.VMEM(...]
where the time goes in v10:
time: 22.3 us; the launch traced here: 22.2 us
  Pallas kernels  21.6 us (97%)
  between operations  0.64 us (3%)
    pallas_call x1, Pallas kernels, local(): pl.pallas_call(body, name='packed_backward', out_shape=tuple((pltpu.VMEM(...  20.8 us
    pallas_call x1, Pallas kernels, local(): pl.pallas_call(store_body, name='store', out_shape=tuple((jax.ShapeDtypeS...  0.81 us

profile of v10, /device:TPU:5, one launch (start us, length us, event | category | flops | bytes accessed | tf_op | source)
XLA Modules:
  0.0 22.2 jit_solution(2895910643833429131)
XLA Ops:
  0.6 20.8 %packed_backward.1 = (bf16[1024,128]{1,0:T(8,128)(2,1)S(1)}, bf16[512,128]{1,0:T(8,128)(2,1)S(1)}, bf16[512,128]{1,0:T(8,128)(2,1)S(1)}) custom-call(s32[14]{0:T(128)} %cu_hbm.1, bf16[1024,128]{1,0:T(8,128)(2,1)} %bitcast.5, bf16[512,128]{1,0:T(8,128)(2,1)} %k_hbm.1, bf16[512,128]{1,0:T(8,128)(2,1)} %v_hbm.1, bf16[1024,128]{1,0:T(8,128)(2,1)} %bitcast.6, ...), custom_call_target="tpu_custom_call" | custom-call | tf_op jit(solution)/shard_map/packed_backward/pallas_call | solution.py:458
  21.4 0.8 %store.1 = (bf16[1024,128]{1,0:T(8,128)(2,1)}, bf16[512,128]{1,0:T(8,128)(2,1)}, bf16[512,128]{1,0:T(8,128)(2,1)}) custom-call(bf16[1024,128]{1,0:T(8,128)(2,1)S(1)} %get-tuple-element.9.dq_ref, bf16[512,128]{1,0:T(8,128)(2,1)S(1)} %get-tuple-element.10.dk_ref, bf16[512,128]{1,0:T(8,128)(2,1)S(1)} %get-tuple-element.11.dv_ref), custom_call_target="tpu_custom_call" | custom-call | tf_op jit(solution)/shard_map/store/pallas_call | solution.py:477

commit v11 on v10

--- a/solution.py
+++ b/solution.py
@@ -35,7 +35,7 @@
     4: (101, 102, 103),
     5: (110, 101, 1, 111, 112, 113, 102, 103),
     6: (111, 112, 113, 101),
-    7: (101, 111, 102, 112, 103),
+    7: (101, 111, 102, 103),
 }
 AFTER = {
     1: (10, 11),
@@ -45,14 +45,14 @@
 LATER = {
     3: (113,),
     6: (102, 103),
-    7: (113,),
+    7: (112, 113),
 }
 TAIL = (2, 3, 0, 0, 2, 3, 0, 0)
 LATE_KEYS = 4
 GO = ((4, 1), (5, 2), (6, 3))
 KV_REL = {(2, 2): (3, 3), (3, 2): (2, 1), (5, 3): (4, 2), (4, 1): (5, 2), (6, 3): (4, 1), (6, 2): (7, 3), (7, 2): (6, 1)}
 QD_REL = {(0, 2): (1, 1), (1, 2): (0, 3), (1, 3): (3, 1), (3, 1): (2, 2), (3, 2): (2, 3), (4, 2): (5, 1), (5, 2): (4, 3)}
-ORDER = ("ghijkoplmqnr", "aobkpqlrghminj", "ghijcadbkolpmqnr", "abcedfsgkhlimjnopqr", "gheijkfolpcabmnqrd", "abkglhecdminfj", "ghijceafsdb", "abcefds")
+ORDER = ("ghijkoplmqnr", "aobkpqlrghminj", "ghijcadbkolpmqnr", "abcedfsgkhlimjnopqr", "gheijkfolpcabmnqrd", "abkglhecdimnfj", "ghijceafsdb", "abcefds")
 
 
 def step_codes(letters):

time: 22.3 us -> 22.5 us (level)
  no operation moved by 1% of the time
where the time goes in v11:
time: 22.5 us; the launch traced here: 22.4 us
  Pallas kernels  21.8 us (97%)
  between operations  0.64 us (3%)
    pallas_call x1, Pallas kernels, local(): pl.pallas_call(body, name='packed_backward', out_shape=tuple((pltpu.VMEM(...  21 us
    pallas_call x1, Pallas kernels, local(): pl.pallas_call(store_body, name='store', out_shape=tuple((jax.ShapeDtypeS...  0.81 us

profile of v11, /device:TPU:5, one launch (start us, length us, event | category | flops | bytes accessed | tf_op | source)
XLA Modules:
  0.0 22.4 jit_solution(2400604985786612276)
XLA Ops:
  0.6 21.0 %packed_backward.1 = (bf16[1024,128]{1,0:T(8,128)(2,1)S(1)}, bf16[512,128]{1,0:T(8,128)(2,1)S(1)}, bf16[512,128]{1,0:T(8,128)(2,1)S(1)}) custom-call(s32[14]{0:T(128)} %cu_hbm.1, bf16[1024,128]{1,0:T(8,128)(2,1)} %bitcast.5, bf16[512,128]{1,0:T(8,128)(2,1)} %k_hbm.1, bf16[512,128]{1,0:T(8,128)(2,1)} %v_hbm.1, bf16[1024,128]{1,0:T(8,128)(2,1)} %bitcast.6, ...), custom_call_target="tpu_custom_call" | custom-call | tf_op jit(solution)/shard_map/packed_backward/pallas_call | solution.py:458
  21.6 0.8 %store.1 = (bf16[1024,128]{1,0:T(8,128)(2,1)}, bf16[512,128]{1,0:T(8,128)(2,1)}, bf16[512,128]{1,0:T(8,128)(2,1)}) custom-call(bf16[1024,128]{1,0:T(8,128)(2,1)S(1)} %get-tuple-element.9.dq_ref, bf16[512,128]{1,0:T(8,128)(2,1)S(1)} %get-tuple-element.10.dk_ref, bf16[512,128]{1,0:T(8,128)(2,1)S(1)} %get-tuple-element.11.dv_ref), custom_call_target="tpu_custom_call" | custom-call | tf_op jit(solution)/shard_map/store/pallas_call | solution.py:477

commit v12 on v10

--- a/solution.py
+++ b/solution.py
@@ -52,7 +52,7 @@
 GO = ((4, 1), (5, 2), (6, 3))
 KV_REL = {(2, 2): (3, 3), (3, 2): (2, 1), (5, 3): (4, 2), (4, 1): (5, 2), (6, 3): (4, 1), (6, 2): (7, 3), (7, 2): (6, 1)}
 QD_REL = {(0, 2): (1, 1), (1, 2): (0, 3), (1, 3): (3, 1), (3, 1): (2, 2), (3, 2): (2, 3), (4, 2): (5, 1), (5, 2): (4, 3)}
-ORDER = ("ghijkoplmqnr", "aobkpqlrghminj", "ghijcadbkolpmqnr", "abcedfsgkhlimjnopqr", "gheijkfolpcabmnqrd", "abkglhecdminfj", "ghijceafsdb", "abcefds")
+ORDER = ("ghijkoplmqnr", "aobkpqlrghminj", "ghijcadbkolpmqnr", "abcedfsgkhlimjnopqr", "gheijkfolpcabmnqrd", "abkglhecdminfj", "ghijcefsadb", "abcefds")
 
 
 def step_codes(letters):
@@ -81,10 +81,10 @@
 
 def body(
     cu_hbm, q_hbm, k_hbm, v_hbm, o_hbm, lse_hbm, do_hbm,
-    dq_out, dk_out, dv_out,
+    dq_out, dk_acc, dv_acc,
     q_loc, k_loc, v_loc, o_loc, lse_loc, do_loc, stat_loc, starts,
     k_buf, v_buf, q_buf, do_buf, stat_buf,
-    dqt, dk_acc, dv_acc, cu_ref, in_sem, go_sem,
+    dqt, cu_ref, in_sem, go_sem,
     k_recv, v_recv, q_recv, do_recv, stat_recv,
     kv_own, qd_own, stat_own, kv_rel, qd_rel, stat_rel,
 ):
@@ -418,9 +418,6 @@
 
     lax.fori_loop(0, steps, step, tuple(packed))
 
-    dk_out[...] = (dk_acc[...] * scale).astype(jnp.bfloat16)
-    dv_out[...] = dv_acc[...].astype(jnp.bfloat16)
-
     def sent(ref, sem):
         pltpu.make_async_remote_copy(src_ref=ref, dst_ref=ref, send_sem=sem, recv_sem=sem, device_id=place(me), device_id_type=MESH).wait_send()
 
@@ -437,11 +434,14 @@
                 sent(stat_loc, stat_sem.at[n])
 
 
-def store_body(dq_ref, dk_ref, dv_ref, dq_out, dk_out, dv_out, sems):
-    pairs = ((dq_ref, dq_out), (dk_ref, dk_out), (dv_ref, dv_out))
+def store_body(dq_ref, dk_ref, dv_ref, dq_out, dk_out, dv_out, dk_st, dv_st, sems):
+    pairs = ((dq_ref, dq_out), (dk_st, dk_out), (dv_st, dv_out))
     copies = [pltpu.make_async_copy(src, dst, sems.at[i]) for i, (src, dst) in enumerate(pairs)]
-    for copy in copies:
-        copy.start()
+    copies[0].start()
+    dk_st[...] = (dk_ref[...] * dk_ref.shape[1] ** -0.5).astype(jnp.bfloat16)
+    copies[1].start()
+    dv_st[...] = dv_ref[...].astype(jnp.bfloat16)
+    copies[2].start()
     for copy in copies:
         copy.wait()
 
@@ -458,7 +458,7 @@
         results = pl.pallas_call(
             body,
             name="packed_backward",
-            out_shape=tuple(pltpu.VMEM(shape, bf) for shape in shapes),
+            out_shape=tuple(pltpu.VMEM(shape, kind) for shape, kind in zip(shapes, (bf, f32, f32))),
             in_specs=[any_spec] * 7,
             out_specs=(vmem_spec,) * 3,
             scratch_shapes=[
@@ -467,7 +467,7 @@
                 pltpu.VMEM((2, qrows), f32), pltpu.VMEM((HOPS + 1, 1, qrows), jnp.int32),
                 pltpu.VMEM((HOPS, rows, head), bf), pltpu.VMEM((HOPS, rows, head), bf),
                 pltpu.VMEM((HOPS, qrows, head), bf), pltpu.VMEM((HOPS, qrows, head), bf), pltpu.VMEM((HOPS, 2, qrows), f32),
-                pltpu.VMEM((head, qrows), f32), pltpu.VMEM((rows, head), f32), pltpu.VMEM((rows, head), f32),
+                pltpu.VMEM((head, qrows), f32),
                 pltpu.SMEM(cu_seqlens.shape, jnp.int32), dma((9,)), pltpu.SemaphoreType.REGULAR,
                 dma((HOPS, NK)), dma((HOPS, NK)), dma((HOPS, NQ)), dma((HOPS, NQ)), dma((HOPS,)),
                 dma((2,)), dma((2,)), dma((2,)), dma((HOPS,)), dma((HOPS,)), dma((HOPS,)),
@@ -480,7 +480,7 @@
             out_shape=tuple(jax.ShapeDtypeStruct(shape, bf) for shape in shapes),
             in_specs=[vmem_spec] * 3,
             out_specs=(any_spec,) * 3,
-            scratch_shapes=[dma((3,))],
+            scratch_shapes=[pltpu.VMEM((rows, head), bf), pltpu.VMEM((rows, head), bf), dma((3,))],
         )(*[pltpu.with_memory_space_constraint(x, pltpu.VMEM) for x in results])
         return d_query.reshape(rows, heads, head), d_key, d_value
 

time: 22.3 us -> 22.3 us (level)
  no operation moved by 1% of the time
where the time goes in v12:
time: 22.3 us; the launch traced here: 22.2 us
  Pallas kernels  21.5 us (96%)
  between operations  0.64 us (3%)
    pallas_call x1, Pallas kernels, local(): pl.pallas_call(body, name='packed_backward', out_shape=tuple((pltpu.VMEM(...  20.7 us
    pallas_call x1, Pallas kernels, local(): pl.pallas_call(store_body, name='store', out_shape=tuple((jax.ShapeDtypeS...  0.81 us

profile of v12, /device:TPU:5, one launch (start us, length us, event | category | flops | bytes accessed | tf_op | source)
XLA Modules:
  0.0 22.2 jit_solution(315363563389915779)
XLA Ops:
  0.6 20.7 %packed_backward.1 = (bf16[1024,128]{1,0:T(8,128)(2,1)S(1)}, f32[512,128]{1,0:T(8,128)S(1)}, f32[512,128]{1,0:T(8,128)S(1)}) custom-call(s32[14]{0:T(128)} %cu_hbm.1, bf16[1024,128]{1,0:T(8,128)(2,1)} %bitcast.5, bf16[512,128]{1,0:T(8,128)(2,1)} %k_hbm.1, bf16[512,128]{1,0:T(8,128)(2,1)} %v_hbm.1, bf16[1024,128]{1,0:T(8,128)(2,1)} %bitcast.6, ...), custom_call_target="tpu_custom_call" | custom-call | tf_op jit(solution)/shard_map/packed_backward/pallas_call | solution.py:458
  21.4 0.8 %store.1 = (bf16[1024,128]{1,0:T(8,128)(2,1)}, bf16[512,128]{1,0:T(8,128)(2,1)}, bf16[512,128]{1,0:T(8,128)(2,1)}) custom-call(bf16[1024,128]{1,0:T(8,128)(2,1)S(1)} %get-tuple-element.9.dq_ref, f32[512,128]{1,0:T(8,128)S(1)} %get-tuple-element.10.dk_ref, f32[512,128]{1,0:T(8,128)S(1)} %get-tuple-element.11.dv_ref), custom_call_target="tpu_custom_call" | custom-call | tf_op jit(solution)/shard_map/store/pallas_call | solution.py:477

commit v13 on v10

--- a/solution.py
+++ b/solution.py
@@ -22,11 +22,11 @@
     0: (0, 10, 1, 11),
     1: (0, 1, 100),
     2: (0, 1, 100),
-    3: (100, 110),
+    3: (110, 100),
     4: (0, 10, 1, 11, 100),
     5: (0, 100),
-    6: (0, 1, 110, 100),
-    7: (100, 110),
+    6: (0, 1, 100, 110),
+    7: (110, 100),
 }
 REST = {
     1: (101, 102, 103),
@@ -64,10 +64,6 @@
     return [p if p == NOBODY else p[0] * 4 + p[1] for p in pairs]
 
 
-def nth(table, n):
-    return [NOBODY if len(table[d]) <= n else table[d][n][0] * 4 + table[d][n][1] for d in range(8)]
-
-
 def partners():
     near = {d: set() for d in range(8)}
     pairs = [(d, target) for table in (KV_OWN, QD_OWN) for d in table for target, _ in table[d]]
@@ -106,13 +102,6 @@
     def place(target):
         return {"cpo": target // 4, "cp": target % 4}
 
-    barrier = pltpu.get_barrier_semaphore()
-    near = partners()
-    for d in range(8):
-        @pl.when(me == d)
-        def _(d=d):
-            for other in [x for x in range(8) if d in near[x]]:
-                pl.semaphore_signal(barrier, inc=1, device_id=place(other), device_id_type=MESH)
     loads = [
         pltpu.make_async_copy(src, dst, in_sem.at[i])
         for i, (src, dst) in enumerate(
@@ -125,6 +114,13 @@
     ]
     for load in loads:
         load.start()
+    barrier = pltpu.get_barrier_semaphore()
+    near = partners()
+    for d in range(8):
+        @pl.when(me == d)
+        def _(d=d):
+            for other in [x for x in range(8) if d in near[x]]:
+                pl.semaphore_signal(barrier, inc=1, device_id=place(other), device_id_type=MESH)
     for d in range(8):
         @pl.when(me == d)
         def _(d=d):
@@ -158,9 +154,6 @@
         return pltpu.make_async_remote_copy(
             src_ref=src, dst_ref=stat_buf.at[there], send_sem=sem, recv_sem=stat_recv.at[there],
             device_id=place(target), device_id_type=MESH)
-
-    kv_to = [lut(nth(KV_OWN, n)) for n in range(2)]
-    qd_to = [lut(nth(QD_OWN, n)) for n in range(2)]
 
     def send(d, item):
         kind, n, chunk = item // 100, item // 10 % 10, item % 10
@@ -424,17 +417,17 @@
     def sent(ref, sem):
         pltpu.make_async_remote_copy(src_ref=ref, dst_ref=ref, send_sem=sem, recv_sem=sem, device_id=place(me), device_id_type=MESH).wait_send()
 
-    for targets, kv_sem in ((kv_to, kv_own), (kv_on, kv_rel)):
-        for n, target in enumerate(targets):
-            @pl.when(target != NOBODY)
-            def _(n=n, kv_sem=kv_sem):
-                sent(q_buf.at[0], kv_sem.at[n])
-    for targets, qd_sem, stat_sem in ((qd_to, qd_own, stat_own), (qd_on, qd_rel, stat_rel)):
-        for n, target in enumerate(targets):
-            @pl.when(target != NOBODY)
-            def _(n=n, qd_sem=qd_sem, stat_sem=stat_sem):
-                sent(q_buf.at[0:2], qd_sem.at[n])
-                sent(stat_loc, stat_sem.at[n])
+    for d in range(8):
+        @pl.when(me == d)
+        def _(d=d):
+            keys_sent = [kv_own.at[n] for n in range(len(KV_OWN[d]))] + [kv_rel.at[h] for h in range(HOPS) if (d, h + 1) in KV_REL]
+            queries_sent = [(qd_own.at[n], stat_own.at[n]) for n in range(len(QD_OWN[d]))]
+            queries_sent += [(qd_rel.at[h], stat_rel.at[h]) for h in range(HOPS) if (d, h + 1) in QD_REL]
+            for sem in keys_sent:
+                sent(q_buf.at[0], sem)
+            for sem, stat_sem in queries_sent:
+                sent(q_buf.at[0:2], sem)
+                sent(stat_loc, stat_sem)
 
 
 def store_body(dq_ref, dk_ref, dv_ref, dq_out, dk_out, dv_out, sems):

time: 22.3 us -> 22.3 us (level)
  no operation moved by 1% of the time
where the time goes in v13:
time: 22.3 us; the launch traced here: 22.2 us
  Pallas kernels  21.5 us (96%)
  between operations  0.64 us (3%)
    pallas_call x1, Pallas kernels, local(): pl.pallas_call(body, name='packed_backward', out_shape=tuple((pltpu.VMEM(...  20.7 us
    pallas_call x1, Pallas kernels, local(): pl.pallas_call(store_body, name='store', out_shape=tuple((jax.ShapeDtypeS...  0.81 us

profile of v13, /device:TPU:5, one launch (start us, length us, event | category | flops | bytes accessed | tf_op | source)
XLA Modules:
  0.0 22.2 jit_solution(13276171183136175704)
XLA Ops:
  0.6 20.7 %packed_backward.1 = (bf16[1024,128]{1,0:T(8,128)(2,1)S(1)}, bf16[512,128]{1,0:T(8,128)(2,1)S(1)}, bf16[512,128]{1,0:T(8,128)(2,1)S(1)}) custom-call(s32[14]{0:T(128)} %cu_hbm.1, bf16[1024,128]{1,0:T(8,128)(2,1)} %bitcast.5, bf16[512,128]{1,0:T(8,128)(2,1)} %k_hbm.1, bf16[512,128]{1,0:T(8,128)(2,1)} %v_hbm.1, bf16[1024,128]{1,0:T(8,128)(2,1)} %bitcast.6, ...), custom_call_target="tpu_custom_call" | custom-call | tf_op jit(solution)/shard_map/packed_backward/pallas_call | solution.py:451
  21.4 0.8 %store.1 = (bf16[1024,128]{1,0:T(8,128)(2,1)}, bf16[512,128]{1,0:T(8,128)(2,1)}, bf16[512,128]{1,0:T(8,128)(2,1)}) custom-call(bf16[1024,128]{1,0:T(8,128)(2,1)S(1)} %get-tuple-element.9.dq_ref, bf16[512,128]{1,0:T(8,128)(2,1)S(1)} %get-tuple-element.10.dk_ref, bf16[512,128]{1,0:T(8,128)(2,1)S(1)} %get-tuple-element.11.dv_ref), custom_call_target="tpu_custom_call" | custom-call | tf_op jit(solution)/shard_map/store/pallas_call | solution.py:470

commit v14 on v13

--- a/solution.py
+++ b/solution.py
@@ -52,7 +52,7 @@
 GO = ((4, 1), (5, 2), (6, 3))
 KV_REL = {(2, 2): (3, 3), (3, 2): (2, 1), (5, 3): (4, 2), (4, 1): (5, 2), (6, 3): (4, 1), (6, 2): (7, 3), (7, 2): (6, 1)}
 QD_REL = {(0, 2): (1, 1), (1, 2): (0, 3), (1, 3): (3, 1), (3, 1): (2, 2), (3, 2): (2, 3), (4, 2): (5, 1), (5, 2): (4, 3)}
-ORDER = ("ghijkoplmqnr", "aobkpqlrghminj", "ghijcadbkolpmqnr", "abcedfsgkhlimjnopqr", "gheijkfolpcabmnqrd", "abkglhecdminfj", "ghijceafsdb", "abcefds")
+ORDER = ("ghijkoplmqnr", "aobkpqlrghminj", "ghijcadbkolpmqnr", "abcedfgkhslimjnopqr", "gheijkfolpcabmnqrd", "abkglhecdminfj", "ghijceafsdb", "abcefds")
 
 
 def step_codes(letters):

time: 22.3 us -> 22.8 us (1.022)
  the two profiles are of different devices: /device:TPU:5 before, /device:TPU:0 now
where the time goes in v14:
time: 22.8 us; the launch traced here: 22.7 us
  Pallas kernels  22.1 us (97%)
  between operations  0.64 us (3%)
    pallas_call x1, Pallas kernels, local(): pl.pallas_call(body, name='packed_backward', out_shape=tuple((pltpu.VMEM(...  21.3 us
    pallas_call x1, Pallas kernels, local(): pl.pallas_call(store_body, name='store', out_shape=tuple((jax.ShapeDtypeS...  0.81 us

profile of v14, /device:TPU:0, one launch (start us, length us, event | category | flops | bytes accessed | tf_op | source)
XLA Modules:
  0.0 22.7 jit_solution(4509746912830745648)
XLA Ops:
  0.6 21.3 %packed_backward.1 = (bf16[1024,128]{1,0:T(8,128)(2,1)S(1)}, bf16[512,128]{1,0:T(8,128)(2,1)S(1)}, bf16[512,128]{1,0:T(8,128)(2,1)S(1)}) custom-call(s32[14]{0:T(128)} %cu_hbm.1, bf16[1024,128]{1,0:T(8,128)(2,1)} %bitcast.5, bf16[512,128]{1,0:T(8,128)(2,1)} %k_hbm.1, bf16[512,128]{1,0:T(8,128)(2,1)} %v_hbm.1, bf16[1024,128]{1,0:T(8,128)(2,1)} %bitcast.6, ...), custom_call_target="tpu_custom_call" | custom-call | tf_op jit(solution)/shard_map/packed_backward/pallas_call | solution.py:451
  21.9 0.8 %store.1 = (bf16[1024,128]{1,0:T(8,128)(2,1)}, bf16[512,128]{1,0:T(8,128)(2,1)}, bf16[512,128]{1,0:T(8,128)(2,1)}) custom-call(bf16[1024,128]{1,0:T(8,128)(2,1)S(1)} %get-tuple-element.9.dq_ref, bf16[512,128]{1,0:T(8,128)(2,1)S(1)} %get-tuple-element.10.dk_ref, bf16[512,128]{1,0:T(8,128)(2,1)S(1)} %get-tuple-element.11.dv_ref), custom_call_target="tpu_custom_call" | custom-call | tf_op jit(solution)/shard_map/store/pallas_call | solution.py:470

commit v15 on v14

--- a/solution.py
+++ b/solution.py
@@ -52,7 +52,7 @@
 GO = ((4, 1), (5, 2), (6, 3))
 KV_REL = {(2, 2): (3, 3), (3, 2): (2, 1), (5, 3): (4, 2), (4, 1): (5, 2), (6, 3): (4, 1), (6, 2): (7, 3), (7, 2): (6, 1)}
 QD_REL = {(0, 2): (1, 1), (1, 2): (0, 3), (1, 3): (3, 1), (3, 1): (2, 2), (3, 2): (2, 3), (4, 2): (5, 1), (5, 2): (4, 3)}
-ORDER = ("ghijkoplmqnr", "aobkpqlrghminj", "ghijcadbkolpmqnr", "abcedfgkhslimjnopqr", "gheijkfolpcabmnqrd", "abkglhecdminfj", "ghijceafsdb", "abcefds")
+ORDER = ("ghijkoplmqnr", "aobkpqlrghminj", "ghijcadbkolpmqnr", "abcedfsgkhlimjnopqr", "gheijkfolpcabmnqdr", "abkglhecdmifnj", "ghijceafsdb", "abcefds")
 
 
 def step_codes(letters):

time: 22.8 us -> 22.3 us (0.978)
  the two profiles are of different devices: /device:TPU:0 before, /device:TPU:5 now
where the time goes in v15:
time: 22.3 us; the launch traced here: 22.2 us
  Pallas kernels  21.5 us (96%)
  between operations  0.64 us (3%)
    pallas_call x1, Pallas kernels, local(): pl.pallas_call(body, name='packed_backward', out_shape=tuple((pltpu.VMEM(...  20.7 us
    pallas_call x1, Pallas kernels, local(): pl.pallas_call(store_body, name='store', out_shape=tuple((jax.ShapeDtypeS...  0.81 us

profile of v15, /device:TPU:5, one launch (start us, length us, event | category | flops | bytes accessed | tf_op | source)
XLA Modules:
  0.0 22.2 jit_solution(13024379920344487134)
XLA Ops:
  0.6 20.7 %packed_backward.1 = (bf16[1024,128]{1,0:T(8,128)(2,1)S(1)}, bf16[512,128]{1,0:T(8,128)(2,1)S(1)}, bf16[512,128]{1,0:T(8,128)(2,1)S(1)}) custom-call(s32[14]{0:T(128)} %cu_hbm.1, bf16[1024,128]{1,0:T(8,128)(2,1)} %bitcast.5, bf16[512,128]{1,0:T(8,128)(2,1)} %k_hbm.1, bf16[512,128]{1,0:T(8,128)(2,1)} %v_hbm.1, bf16[1024,128]{1,0:T(8,128)(2,1)} %bitcast.6, ...), custom_call_target="tpu_custom_call" | custom-call | tf_op jit(solution)/shard_map/packed_backward/pallas_call | solution.py:451
  21.4 0.8 %store.1 = (bf16[1024,128]{1,0:T(8,128)(2,1)}, bf16[512,128]{1,0:T(8,128)(2,1)}, bf16[512,128]{1,0:T(8,128)(2,1)}) custom-call(bf16[1024,128]{1,0:T(8,128)(2,1)S(1)} %get-tuple-element.9.dq_ref, bf16[512,128]{1,0:T(8,128)(2,1)S(1)} %get-tuple-element.10.dk_ref, bf16[512,128]{1,0:T(8,128)(2,1)S(1)} %get-tuple-element.11.dv_ref), custom_call_target="tpu_custom_call" | custom-call | tf_op jit(solution)/shard_map/store/pallas_call | solution.py:470

commit v16 on v15

--- a/solution.py
+++ b/solution.py
@@ -52,7 +52,7 @@
 GO = ((4, 1), (5, 2), (6, 3))
 KV_REL = {(2, 2): (3, 3), (3, 2): (2, 1), (5, 3): (4, 2), (4, 1): (5, 2), (6, 3): (4, 1), (6, 2): (7, 3), (7, 2): (6, 1)}
 QD_REL = {(0, 2): (1, 1), (1, 2): (0, 3), (1, 3): (3, 1), (3, 1): (2, 2), (3, 2): (2, 3), (4, 2): (5, 1), (5, 2): (4, 3)}
-ORDER = ("ghijkoplmqnr", "aobkpqlrghminj", "ghijcadbkolpmqnr", "abcedfsgkhlimjnopqr", "gheijkfolpcabmnqdr", "abkglhecdmifnj", "ghijceafsdb", "abcefds")
+ORDER = ("ghijkoplmqnr", "aobkpqlrghminj", "ghijcadbkolpmqnr", "abcedfsgkhlimjnopqr", "gheijkfolpcabmnqdr", "abkglhecdmifnj", "ghijceafsdb", "abcefsd")
 
 
 def step_codes(letters):

time: 22.3 us -> 22.3 us (level)
  no operation moved by 1% of the time
where the time goes in v16:
time: 22.3 us; the launch traced here: 22.2 us
  Pallas kernels  21.5 us (96%)
  between operations  0.64 us (3%)
    pallas_call x1, Pallas kernels, local(): pl.pallas_call(body, name='packed_backward', out_shape=tuple((pltpu.VMEM(...  20.7 us
    pallas_call x1, Pallas kernels, local(): pl.pallas_call(store_body, name='store', out_shape=tuple((jax.ShapeDtypeS...  0.81 us

profile of v16, /device:TPU:5, one launch (start us, length us, event | category | flops | bytes accessed | tf_op | source)
XLA Modules:
  0.0 22.2 jit_solution(2967616661390764678)
XLA Ops:
  0.6 20.7 %packed_backward.1 = (bf16[1024,128]{1,0:T(8,128)(2,1)S(1)}, bf16[512,128]{1,0:T(8,128)(2,1)S(1)}, bf16[512,128]{1,0:T(8,128)(2,1)S(1)}) custom-call(s32[14]{0:T(128)} %cu_hbm.1, bf16[1024,128]{1,0:T(8,128)(2,1)} %bitcast.5, bf16[512,128]{1,0:T(8,128)(2,1)} %k_hbm.1, bf16[512,128]{1,0:T(8,128)(2,1)} %v_hbm.1, bf16[1024,128]{1,0:T(8,128)(2,1)} %bitcast.6, ...), custom_call_target="tpu_custom_call" | custom-call | tf_op jit(solution)/shard_map/packed_backward/pallas_call | solution.py:451
  21.4 0.8 %store.1 = (bf16[1024,128]{1,0:T(8,128)(2,1)}, bf16[512,128]{1,0:T(8,128)(2,1)}, bf16[512,128]{1,0:T(8,128)(2,1)}) custom-call(bf16[1024,128]{1,0:T(8,128)(2,1)S(1)} %get-tuple-element.9.dq_ref, bf16[512,128]{1,0:T(8,128)(2,1)S(1)} %get-tuple-element.10.dk_ref, bf16[512,128]{1,0:T(8,128)(2,1)S(1)} %get-tuple-element.11.dv_ref), custom_call_target="tpu_custom_call" | custom-call | tf_op jit(solution)/shard_map/store/pallas_call | solution.py:470
